TPU v7x, 32 devices: a whole 2x2x4 slice. The times are simulated.
32 devices in a mesh: expert: 16 (over z, y, x), tensor: 2 (over core).
Axes of the slice: x: 2, y: 2, z: 4, core: 2. Of those that a mesh axis runs over, the one named last changes fastest.
Arguments:
- tokens: bfloat16 [8192, 2048], P('expert'), may hold values from -6 to 6
- attn_gain: bfloat16 [2048], P('expert'), may hold values from 0.099609375 to 1.8984375
- moe_gain: bfloat16 [2048], P('expert'), may hold values from 0.099609375 to 1.8984375
- query_gain: bfloat16 [128], P('expert'), may hold values from 0.5 to 4.5
- key_gain: bfloat16 [128], P('expert'), may hold values from 0.5 to 4.5
- query_weight: bfloat16 [2048, 4096], P('expert', 'tensor'), may hold values from -0.088388348 to 0.088388348
- key_weight: bfloat16 [2048, 512], P('expert', 'tensor'), may hold values from -0.088388348 to 0.088388348
- value_matrix: bfloat16 [2048, 512], P('expert', 'tensor'), may hold values from -0.125 to 0.125
- output_weight: bfloat16 [2048, 4096], P('expert', 'tensor'), may hold values from -0.375 to 0.375
- gate_proj: bfloat16 [32, 2048, 768], P('expert', None, 'tensor'), may hold values from -0.125 to 0.125
- up_proj: bfloat16 [32, 2048, 768], P('expert', None, 'tensor'), may hold values from -0.125 to 0.125
- down_proj: bfloat16 [32, 768, 2048], P('expert', 'tensor'), may hold values from -0.875 to 0.875
- gate_weights: float32 [8192, 8], P('expert'), may hold values from 0.05 to 0.25
- routes: int32 [8192, 8], P('expert'), may hold values from 0 to 31, all different within a row; in each aligned block of 512 rows (0 to 511, 512 to 1023, ...) at most 160 rows name the same one
- doc_start: int32 [8192], P('expert'), may hold values from 0 to 1, as said below
- cotangent: bfloat16 [8192, 2048], P('expert'), may hold values from -6 to 6
Outputs:
- block_out: bfloat16 [8192, 2048], P('expert')
- grad_tokens: float32 [8192, 2048], P('expert')
- grad_query: float32 [2048, 4096], P('expert', 'tensor')
- grad_key: float32 [2048, 512], P('expert', 'tensor')
- grad_value: float32 [2048, 512], P('expert', 'tensor')
- grad_output: float32 [2048, 4096], P('expert', 'tensor')
- grad_attn_gain: float32 [2048], P('expert')
- grad_moe_gain: float32 [2048], P('expert')
- grad_query_gain: float32 [128], P('expert')
- grad_key_gain: float32 [128], P('expert')
- grad_gate_proj: float32 [32, 2048, 768], P('expert', None, 'tensor')
- grad_up_proj: float32 [32, 2048, 768], P('expert', None, 'tensor')
- grad_down_proj: float32 [32, 768, 2048], P('expert', 'tensor')
- grad_gates: float32 [8192, 8], P('expert')
Inputs may be any that keep to these rules, and one draw needn't show every extreme that they name: `routes`: in each device's 512 rows no expert is named by more than 160 rows, a bound that some block reaches. `doc_start`: each block of 512 rows begins with 1, so documents never cross blocks; some block holds a single document of 512 rows.
All inputs are finite; a program needn't handle non-finite values.
Results may differ from a plain program's by a relative error of at most 0.015.
The roundings to bfloat16 on the way count: a program that leaves them out, or rounds other values in their place, can miss the bound.
Values may be sent and summed in bfloat16 or wider, within the bound.
A program may use at most 384 MiB of HBM per device.

v0:
```python
import jax
import jax.numpy as jnp
from jax import lax
from jax.sharding import PartitionSpec as P

HEAD_SIZE = 128


EPS = 1e-06
NEG = -1e30
THETA = 1000000.0


def rms_parts(value_heads_out):
    factor = lax.rsqrt(jnp.mean(value_heads_out * value_heads_out, axis=-1, keepdims=True) + EPS)
    return (value_heads_out * factor, factor)


def norm_back(grad_unit, unit_value, factor):
    return factor * (
        grad_unit - unit_value * jnp.mean(grad_unit * unit_value, axis=-1, keepdims=True)
    )


def rotate(value_heads_out, cos_table, sin_table):
    half_dim = value_heads_out.shape[-1] // 2
    lower_half = value_heads_out[..., :half_dim]
    upper_half = value_heads_out[..., half_dim:]
    return jnp.concatenate(
        [
            lower_half * cos_table - upper_half * sin_table,
            upper_half * cos_table + lower_half * sin_table,
        ],
        axis=-1,
    )


def doc_tables(doc_start):
    row_count = doc_start.shape[0]
    places = jnp.arange(row_count, dtype=jnp.int32)
    begins = lax.cummax(jnp.where(doc_start == 1, places, 0), axis=0)
    offset = (places - begins).astype(jnp.float32)
    frequency = THETA ** (-(jnp.arange(HEAD_SIZE // 2, dtype=jnp.float32) * 2.0 / HEAD_SIZE))
    angles = offset[:, None] * frequency[None, :]
    document_index = jnp.cumsum(doc_start)
    allowed = (document_index[:, None] == document_index[None, :]) & (
        places[:, None] >= places[None, :]
    )
    return (jnp.cos(angles)[:, None, :], jnp.sin(angles)[:, None, :], allowed)


def scores_of(grouped_heads, keys_low, allowed):
    scaled = jnp.einsum(
        "qngd,knd->ngqk", grouped_heads, keys_low, preferred_element_type=jnp.float32
    ) * HEAD_SIZE ** (-0.5)
    return jnp.where(allowed, scaled, NEG)


def to_owners(fetcher, experts, capacity):
    picked = fetcher(jnp.arange(experts * capacity, dtype=jnp.int32)).reshape(experts, capacity, -1)
    arrived = lax.all_to_all(picked, "expert", split_axis=0, concat_axis=0, tiled=True)
    return arrived


def to_sources(expert_rows, places_sent):
    width = expert_rows.shape[-1]
    returned = lax.all_to_all(expert_rows, "expert", split_axis=0, concat_axis=0, tiled=True)
    return returned.reshape(-1, width)[places_sent].astype(jnp.float32)


def local(
    tokens,
    attn_gain,
    moe_gain,
    query_gain,
    key_gain,
    query_weight,
    key_weight,
    value_matrix,
    output_weight,
    gate_proj,
    up_proj,
    down_proj,
    gate_weights,
    routes,
    doc_start,
    cotangent,
):
    gathered = (
        lax.all_gather(query_weight, "expert", axis=0, tiled=True),
        lax.all_gather(key_weight, "expert", axis=0, tiled=True),
        lax.all_gather(value_matrix, "expert", axis=0, tiled=True),
        lax.all_gather(output_weight, "expert", axis=0, tiled=True),
        lax.all_gather(attn_gain, "expert", axis=0, tiled=True),
        lax.all_gather(moe_gain, "expert", axis=0, tiled=True),
        lax.all_gather(query_gain, "expert", axis=0, tiled=True),
        lax.all_gather(key_gain, "expert", axis=0, tiled=True),
    )
    full_query, full_key, full_value, full_output = (
        gathered[0],
        gathered[1],
        gathered[2],
        gathered[3],
    )
    gain_attn = gathered[4].astype(jnp.float32)
    gain_moe = gathered[5].astype(jnp.float32)
    gain_query = gathered[6].astype(jnp.float32)
    gain_key = gathered[7].astype(jnp.float32)
    cos_table, sin_table, allowed = doc_tables(doc_start)
    tok_rows = tokens.shape[0]
    heads_here = full_query.shape[1] // HEAD_SIZE
    kv_here = full_key.shape[1] // HEAD_SIZE
    query_group_width = heads_here // kv_here
    inputs = tokens.astype(jnp.float32)
    unit_attn, factor_attn = rms_parts(inputs)
    normalized_input = (unit_attn * gain_attn).astype(jnp.bfloat16)
    query_raw = jnp.dot(normalized_input, full_query, preferred_element_type=jnp.float32).reshape(
        tok_rows, heads_here, HEAD_SIZE
    )
    key_unrotated = jnp.dot(normalized_input, full_key, preferred_element_type=jnp.float32).reshape(
        tok_rows, kv_here, HEAD_SIZE
    )
    values_low = (
        jnp.dot(normalized_input, full_value, preferred_element_type=jnp.float32)
        .astype(jnp.bfloat16)
        .reshape(tok_rows, kv_here, HEAD_SIZE)
    )
    query_unit, query_factor = rms_parts(query_raw)
    key_unit, key_factor = rms_parts(key_unrotated)
    queries_low = rotate(query_unit * gain_query, cos_table, sin_table).astype(jnp.bfloat16)
    keys_low = rotate(key_unit * gain_key, cos_table, sin_table).astype(jnp.bfloat16)
    grouped_heads = queries_low.reshape(tok_rows, kv_here, query_group_width, HEAD_SIZE)
    scores = scores_of(grouped_heads, keys_low, allowed)
    row_peak = jnp.max(scores, axis=-1, keepdims=True)
    weights = jnp.exp(scores - row_peak)
    totals = jnp.sum(weights, axis=-1, keepdims=True)
    probs_low = (weights / totals).astype(jnp.bfloat16)
    log_total = row_peak + jnp.log(totals)
    mixed_low = (
        jnp.einsum("ngqk,knd->qngd", probs_low, values_low, preferred_element_type=jnp.float32)
        .reshape(tok_rows, heads_here * HEAD_SIZE)
        .astype(jnp.bfloat16)
    )
    attn_part = jnp.einsum("th,dh->td", mixed_low, full_output, preferred_element_type=jnp.float32)
    hidden = inputs + lax.psum(attn_part, "tensor")
    unit_moe, factor_moe = rms_parts(hidden)
    normed_moe = (unit_moe * gain_moe).astype(jnp.bfloat16)
    n_devices = lax.axis_size("expert")
    local_experts = gate_proj.shape[0]
    experts = n_devices * local_experts
    top_count = routes.shape[1]
    assigned = tok_rows * top_count
    capacity = assigned * 5 // (4 * experts)
    chosen = routes.reshape(assigned)
    onehot = (chosen[:, None] == jnp.arange(experts, dtype=jnp.int32)[None, :]).astype(jnp.int32)
    slot_of = jnp.sum((jnp.cumsum(onehot, axis=0) - onehot) * onehot, axis=1)
    places_sent = chosen * capacity + slot_of
    slot_owner = (
        jnp.full((experts * capacity,), assigned, jnp.int32)
        .at[places_sent]
        .set(jnp.arange(assigned, dtype=jnp.int32))
    )
    normed_pad = jnp.concatenate(
        [normed_moe, jnp.zeros((1, normed_moe.shape[1]), jnp.bfloat16)], axis=0
    )

    def fetch_rows(slot_ids):
        return normed_pad[slot_owner[slot_ids] // top_count]

    arrived = to_owners(fetch_rows, experts, capacity).reshape(
        n_devices, local_experts, capacity, -1
    )
    gate_value = jnp.einsum(
        "sled,ldf->slef", arrived, gate_proj, preferred_element_type=jnp.float32
    )
    up_value = jnp.einsum("sled,ldf->slef", arrived, up_proj, preferred_element_type=jnp.float32)
    hidden_act = (jax.nn.silu(gate_value) * up_value).astype(jnp.bfloat16)
    out_rows = jnp.einsum(
        "slef,lfd->sled", hidden_act, down_proj, preferred_element_type=jnp.float32
    ).astype(jnp.bfloat16)
    per_choice = to_sources(out_rows.reshape(experts, capacity, -1), places_sent).reshape(
        tok_rows, top_count, -1
    )
    moe_part = jnp.sum(gate_weights[:, :, None] * per_choice, axis=1)
    moe_out = lax.psum(moe_part.astype(jnp.bfloat16), "tensor").astype(jnp.float32)
    block_out = (hidden + moe_out).astype(jnp.bfloat16)
    upstream = cotangent.astype(jnp.float32)
    gate_part = jnp.sum(per_choice * upstream[:, None, :], axis=-1)
    cot_pad = jnp.concatenate([cotangent, jnp.zeros((1, cotangent.shape[1]), jnp.bfloat16)], axis=0)
    weight_pad = jnp.concatenate(
        [gate_weights.reshape(assigned), jnp.zeros((1,), jnp.float32)], axis=0
    )

    def fetch_grads(slot_ids):
        chosen_slot = slot_owner[slot_ids]
        return (
            weight_pad[chosen_slot][:, None] * cot_pad[chosen_slot // top_count].astype(jnp.float32)
        ).astype(jnp.bfloat16)

    grad_rows = to_owners(fetch_grads, experts, capacity).reshape(
        n_devices, local_experts, capacity, -1
    )
    grad_act = jnp.einsum(
        "sled,lfd->slef", grad_rows, down_proj, preferred_element_type=jnp.float32
    )
    grad_down = jnp.einsum(
        "slef,sled->lfd", hidden_act, grad_rows, preferred_element_type=jnp.float32
    )
    sigmoid_gate = jax.nn.sigmoid(gate_value)
    grad_up_low = (grad_act * gate_value * sigmoid_gate).astype(jnp.bfloat16)
    grad_gate_low = (
        grad_act * up_value * sigmoid_gate * (1.0 + gate_value * (1.0 - sigmoid_gate))
    ).astype(jnp.bfloat16)
    grad_gate_w = jnp.einsum(
        "sled,slef->ldf", arrived, grad_gate_low, preferred_element_type=jnp.float32
    )
    grad_up_w = jnp.einsum(
        "sled,slef->ldf", arrived, grad_up_low, preferred_element_type=jnp.float32
    )
    grad_in = jnp.einsum(
        "slef,ldf->sled", grad_gate_low, gate_proj, preferred_element_type=jnp.float32
    )
    grad_in = (
        grad_in
        + jnp.einsum("slef,ldf->sled", grad_up_low, up_proj, preferred_element_type=jnp.float32)
    ).astype(jnp.bfloat16)
    grad_choice = to_sources(grad_in.reshape(experts, capacity, -1), places_sent).reshape(
        tok_rows, top_count, -1
    )
    grad_moe_part = jnp.sum(grad_choice, axis=1)
    grad_normed_moe, grad_gates = lax.psum((grad_moe_part, gate_part), "tensor")
    grad_moe_gain = jnp.sum(grad_normed_moe * unit_moe, axis=0)
    grad_hidden = upstream + norm_back(grad_normed_moe * gain_moe, unit_moe, factor_moe)
    grad_attn_low = grad_hidden.astype(jnp.bfloat16)
    back_query, back_key, back_value, back_output = (full_query, full_key, full_value, full_output)
    grad_mixed = jnp.einsum(
        "td,dh->th", grad_attn_low, back_output, preferred_element_type=jnp.float32
    )
    grad_mixed_low = grad_mixed.astype(jnp.bfloat16).reshape(
        tok_rows, kv_here, query_group_width, HEAD_SIZE
    )
    grad_output_w = jnp.einsum(
        "td,th->dh", grad_attn_low, mixed_low, preferred_element_type=jnp.float32
    )
    scores = scores_of(grouped_heads, keys_low, allowed)
    prob_full = jnp.exp(scores - log_total)
    grad_probs = jnp.einsum(
        "qngd,knd->ngqk", grad_mixed_low, values_low, preferred_element_type=jnp.float32
    )
    grad_values = jnp.einsum(
        "ngqk,qngd->knd",
        prob_full.astype(jnp.bfloat16),
        grad_mixed_low,
        preferred_element_type=jnp.float32,
    ).astype(jnp.bfloat16)
    row_delta = jnp.sum(prob_full * grad_probs, axis=-1, keepdims=True)
    grad_scores = (prob_full * (grad_probs - row_delta)).astype(jnp.bfloat16)
    score_scale = HEAD_SIZE ** (-0.5)
    grad_queries = (
        jnp.einsum(
            "ngqk,knd->qngd", grad_scores, keys_low, preferred_element_type=jnp.float32
        ).reshape(tok_rows, heads_here, HEAD_SIZE)
        * score_scale
    )
    grad_keys = (
        jnp.einsum("ngqk,qngd->knd", grad_scores, grouped_heads, preferred_element_type=jnp.float32)
        * score_scale
    )
    grad_qhead = rotate(grad_queries, cos_table, -sin_table)
    grad_khead = rotate(grad_keys, cos_table, -sin_table)
    query_gain_part = jnp.sum(grad_qhead * query_unit, axis=(0, 1))
    key_gain_part = jnp.sum(grad_khead * key_unit, axis=(0, 1))
    grad_query_low = (
        norm_back(grad_qhead * gain_query, query_unit, query_factor)
        .astype(jnp.bfloat16)
        .reshape(tok_rows, heads_here * HEAD_SIZE)
    )
    grad_key_low = (
        norm_back(grad_khead * gain_key, key_unit, key_factor)
        .astype(jnp.bfloat16)
        .reshape(tok_rows, kv_here * HEAD_SIZE)
    )
    grad_value_low = grad_values.reshape(tok_rows, kv_here * HEAD_SIZE)
    grad_normed_part = jnp.einsum(
        "th,dh->td", grad_query_low, back_query, preferred_element_type=jnp.float32
    )
    grad_normed_part = grad_normed_part + jnp.einsum(
        "th,dh->td", grad_key_low, back_key, preferred_element_type=jnp.float32
    )
    grad_normed_part = grad_normed_part + jnp.einsum(
        "th,dh->td", grad_value_low, back_value, preferred_element_type=jnp.float32
    )
    grad_query_w = jnp.einsum(
        "td,th->dh", normalized_input, grad_query_low, preferred_element_type=jnp.float32
    )
    grad_key_w = jnp.einsum(
        "td,th->dh", normalized_input, grad_key_low, preferred_element_type=jnp.float32
    )
    grad_value_w = jnp.einsum(
        "td,th->dh", normalized_input, grad_value_low, preferred_element_type=jnp.float32
    )
    grad_normed, query_gain_sum, key_gain_sum = (
        lax.psum(grad_normed_part.astype(jnp.bfloat16), "tensor").astype(jnp.float32),
        lax.psum(query_gain_part.astype(jnp.bfloat16), "tensor").astype(jnp.float32),
        lax.psum(key_gain_part.astype(jnp.bfloat16), "tensor").astype(jnp.float32),
    )
    grad_attn_gain_part = jnp.sum(grad_normed * unit_attn, axis=0)
    grad_tokens = grad_hidden + norm_back(grad_normed * gain_attn, unit_attn, factor_attn)
    shares = (
        lax.psum_scatter(grad_query_w, "expert", scatter_dimension=0, tiled=True),
        lax.psum_scatter(grad_key_w, "expert", scatter_dimension=0, tiled=True),
        lax.psum_scatter(grad_value_w, "expert", scatter_dimension=0, tiled=True),
        lax.psum_scatter(grad_output_w, "expert", scatter_dimension=0, tiled=True),
        lax.psum_scatter(grad_attn_gain_part, "expert", scatter_dimension=0, tiled=True),
        lax.psum_scatter(grad_moe_gain, "expert", scatter_dimension=0, tiled=True),
        lax.psum_scatter(query_gain_sum, "expert", scatter_dimension=0, tiled=True),
        lax.psum_scatter(key_gain_sum, "expert", scatter_dimension=0, tiled=True),
    )
    return (
        block_out,
        grad_tokens,
        shares[0],
        shares[1],
        shares[2],
        shares[3],
        shares[4],
        shares[5],
        shares[6],
        shares[7],
        grad_gate_w,
        grad_up_w,
        grad_down,
        grad_gates,
    )


def solution(mesh):
    return jax.shard_map(
        local,
        mesh=mesh,
        in_specs=(
            P("expert", None),
            P("expert"),
            P("expert"),
            P("expert"),
            P("expert"),
            P("expert", "tensor"),
            P("expert", "tensor"),
            P("expert", "tensor"),
            P("expert", "tensor"),
            P("expert", None, "tensor"),
            P("expert", None, "tensor"),
            P("expert", "tensor", None),
            P("expert", None),
            P("expert", None),
            P("expert"),
            P("expert", None),
        ),
        out_specs=(
            P("expert", None),
            P("expert", None),
            P("expert", "tensor"),
            P("expert", "tensor"),
            P("expert", "tensor"),
            P("expert", "tensor"),
            P("expert"),
            P("expert"),
            P("expert"),
            P("expert"),
            P("expert", None, "tensor"),
            P("expert", None, "tensor"),
            P("expert", "tensor", None),
            P("expert", None),
        ),
        check_vma=False,
    )
```

profile of v0, /device:TPU:10, one launch (start us, length us, event | category | flops | bytes accessed | tf_op | source)
XLA Modules:
  0.0 3590.9 jit_solution(6314324456832241976)
XLA Ops:
  13.7 31.1 all-reduce.9
  47.1 40.9 %all-gather = bf16[16,1,128]{2,1,0:T(2,128)(2,1)S(1)} all-gather(bf16[1,1,128]{2,1,0:T(2,128)(2,1)} %bitcast.317), channel_id=1, replica_groups=mesh['expert'=16,'tensor'=2] {'expert'}, dimensions={0}, use_global_device_ids=true | all-gather | bytes 4352 | tf_op jit(solution)/shard_map/all_gather | solution.py:94
  102.8 20.2 all-gather.7.cloned.1.call-done
  126.5 110.3 %all-gather.11.cloned.1.call-done = bf16[2048,2048]{1,0:T(8,128)(2,1)} async-done(((bf16[128,2048]{1,0:T(8,128)(2,1)}), bf16[2048,2048]{1,0:T(8,128)(2,1)}) %all-gather.11.cloned.1.call-update) | async-done | bytes 8388624 | tf_op jit(solution)/shard_map/all_gather | solution.py:90
  281.4 68.5 %all-gather.13.cloned.1.call-done = bf16[2048,2048]{1,0:T(8,128)(2,1)} async-done(((bf16[128,2048]{1,0:T(8,128)(2,1)}), bf16[2048,2048]{1,0:T(8,128)(2,1)}) %all-gather.13.cloned.1.call-update) | async-done | bytes 8388624 | tf_op jit(solution)/shard_map/all_gather | solution.py:93
  361.7 30.8 all-gather.1
  431.7 28.7 gather_fusion
  468.0 40.7 %gather_fusion.1 = bf16[5120,2048]{1,0:T(8,128)(2,1)} fusion(bf16[513,2048]{1,0:T(8,128)(2,1)} %concatenate.36, s32[5120]{0:T(1024)S(1)} %broadcast_clamp_fusion.1), kind=kCustom, calls=%fused_computation.1 | custom fusion | bytes 41963520 | tf_op jit(solution)/shard_map/gather | solution.py:168
  523.6 28.7 gather_fusion.3
  555.5 40.7 %gather_fusion.4 = bf16[5120,2048]{1,0:T(8,128)(2,1)} fusion(bf16[513,2048]{1,0:T(8,128)(2,1)} %concatenate.38, s32[5120]{0:T(1024)S(1)} %broadcast_clamp_fusion.1), kind=kCustom, calls=%fused_computation.4 | custom fusion | bytes 41963520 | tf_op jit(solution)/shard_map/gather | solution.py:197
  596.2 18.3 fusion
  614.5 367.8 %all-to-all-done = bf16[32,160,2048]{2,1,0:T(8,128)(2,1)} async-done(((bf16[32,160,2048]{2,1,0:T(8,128)(2,1)}), bf16[32,160,2048]{2,1,0:T(8,128)(2,1)}, u32[]{:S(2)}, u32[]{:S(2)}) %all-to-all-start) | async-done | bytes 20971552 | tf_op jit(solution)/shard_map/all_to_all | solution.py:61
  1025.9 433.9 %all-to-all-done.2 = bf16[32,160,2048]{2,1,0:T(8,128)(2,1)} async-done(((bf16[32,160,2048]{2,1,0:T(8,128)(2,1)}), bf16[32,160,2048]{2,1,0:T(8,128)(2,1)}, u32[]{:S(2)}, u32[]{:S(2)}) %all-to-all-start.2) | async-done | bytes 20971552 | tf_op jit(solution)/shard_map/all_to_all | solution.py:61
  1459.8 22.4 fusion.22
  1482.2 21.7 fusion.58
  1504.0 24.7 fusion.3
  1587.9 435.8 %all-to-all-done.3 = bf16[32,160,2048]{2,1,0:T(8,128)(2,1)} async-done(((bf16[32,160,2048]{2,1,0:T(8,128)(2,1)}), bf16[32,160,2048]{2,1,0:T(8,128)(2,1)}, u32[]{:S(2)}, u32[]{:S(2)}) %all-to-all-start.3) | async-done | bytes 20971552 | tf_op jit(solution)/shard_map/all_to_all | solution.py:67
  2033.6 41.0 %gather_fusion.5 = bf16[4096,2048]{1,0:T(8,128)(2,1)} fusion(bf16[5120,2048]{1,0:T(8,128)(2,1)} %bitcast.48, s32[4096]{0:T(1024)S(1)} %broadcast_clamp_fusion.2), kind=kCustom, calls=%fused_computation.5 | custom fusion | bytes 33570816 | tf_op jit(solution)/shard_map/gather | solution.py:68
  2094.1 415.2 %all-to-all-done.1 = bf16[32,160,2048]{2,1,0:T(8,128)(2,1)} async-done(((bf16[32,160,2048]{2,1,0:T(8,128)(2,1)}), bf16[32,160,2048]{2,1,0:T(8,128)(2,1)}, u32[]{:S(2)}, u32[]{:S(2)}) %all-to-all-start.1) | async-done | bytes 20971552 | tf_op jit(solution)/shard_map/all_to_all | solution.py:67
  2509.3 41.3 %gather_fusion.2 = bf16[4096,2048]{1,0:T(8,128)(2,1)} fusion(bf16[5120,2048]{1,0:T(8,128)(2,1)} %bitcast.37, s32[4096]{0:T(1024)S(1)} %broadcast_clamp_fusion.2), kind=kCustom, calls=%fused_computation.2 | custom fusion | bytes 33570816 | tf_op jit(solution)/shard_map/gather | solution.py:68
  2746.5 18.2 fusion.50
  2775.0 65.1 %all-reduce.8 = (f32[2048]{0:T(1024)S(1)}, f32[2048]{0:T(1024)S(1)}, f32[128]{0:T(128)S(1)}, f32[128]{0:T(128)S(1)}) all-reduce(f32[2048]{0:T(1024)S(1)} %get-tuple-element.46, f32[2048]{0:T(1024)S(1)} %copy-done.53, bf16[128]{0:T(256)(128)(2,1)S(1)} %get-tuple-element.54, ...), channel_id=6, replica_groups=mesh['expert'=16,'tensor'=2] {'expert'}, use_global_device_ids=true, to_apply=%region_30.31.clone | all-reduce | flops 4352 | bytes 34304
  2867.5 361.8 %reduce-scatter.11.cloned.1.call-done = f32[128,2048]{1,0:T(8,128)} async-done(((f32[2048,2048]{1,0:T(8,128)}), f32[128,2048]{1,0:T(8,128)}) %reduce-scatter.11.cloned.1.call-update) | async-done | bytes 1048592 | tf_op jit(solution)/shard_map/reduce_scatter | solution.py:313
  3229.3 355.0 %reduce-scatter.5.cloned.1.call-done = f32[128,2048]{1,0:T(8,128)} async-done(((f32[2048,2048]{1,0:T(8,128)}), f32[128,2048]{1,0:T(8,128)}) %reduce-scatter.5.cloned.1.call-update) | async-done | bytes 1048592 | tf_op jit(solution)/shard_map/reduce_scatter | solution.py:310
  (296 shorter events, 511.1 us)
Async XLA Ops:
  7.2 1452.6 %copy-start = (bf16[2,384,2048]{2,1,0:T(8,128)(2,1)S(1)}, bf16[2,384,2048]{2,1,0:T(8,128)(2,1)}, u32[]{:S(2)}) copy-start(bf16[2,384,2048]{2,1,0:T(8,128)(2,1)} %param.27) | copy-start | bytes 9437188
  7.2 86.0 %all-gather.9.cloned.1.call-start = ((), (), s32[]{:S(2)}) async-start(), calls=%async_computation.9 | async-start | bytes 1114112 | tf_op jit(solution)/shard_map/all_gather | solution.py:91
  7.9 115.0 %all-gather.7.cloned.1.call-start = ((), (), s32[]{:S(2)}) async-start(), calls=%async_computation.8 | async-start | bytes 1114112 | tf_op jit(solution)/shard_map/all_gather | solution.py:92
  8.7 228.1 %all-gather.11.cloned.1.call-start = ((), (), s32[]{:S(2)}) async-start(), calls=%async_computation.10 | async-start | bytes 8912896 | tf_op jit(solution)/shard_map/all_gather | solution.py:90
  9.4 340.5 %all-gather.13.cloned.1.call-start = ((), (), s32[]{:S(2)}) async-start(), calls=%async_computation.11 | async-start | bytes 8912896 | tf_op jit(solution)/shard_map/all_gather | solution.py:93
  10.0 450.6 %all-reduce.16.cloned.1.call-start = ((), (), s32[]{:S(2)}) async-start(), calls=%async_computation.12 | async-start | bytes 8388608 | tf_op jit(solution)/shard_map/psum | solution.py:145
  44.9 202.8 %copy-start.59 = (f32[128]{0:T(128)}, f32[128]{0:T(128)S(1)}, u32[]{:S(2)}) copy-start(f32[128]{0:T(128)S(1)} %convert_element_type.165) | copy-start | bytes 1540
  44.9 54.1 %copy-start.61 = (f32[128]{0:T(128)}, f32[128]{0:T(128)S(1)}, u32[]{:S(2)}) copy-start(f32[128]{0:T(128)S(1)} %convert_element_type.163) | copy-start | bytes 1540
  88.0 148.8 %copy-start.46 = (f32[16,1,128]{2,1,0:T(1,128)}, f32[16,1,128]{2,1,0:T(1,128)S(1)}, u32[]{:S(2)}) copy-start(f32[16,1,128]{2,1,0:T(1,128)S(1)} %convert_element_type.209) | copy-start | bytes 24580
  90.3 146.5 %copy-start.56 = (f32[512]{0:T(512)}, f32[512]{0:T(512)S(1)}, u32[]{:S(2)}) copy-start(f32[512]{0:T(512)S(1)} %add_rsqrt_fusion.3) | copy-start | bytes 6148
  93.2 157.4 %copy-start.16 = (f32[512,64]{1,0:T(8,128)}, f32[512,64]{1,0:T(8,128)S(1)}, u32[]{:S(2)}) copy-start(f32[512,64]{1,0:T(8,128)S(1)} %get-tuple-element.87) | copy-start | bytes 393220
  392.5 71.6 %copy-start.44 = (f32[16,1,128]{2,1,0:T(1,128)}, f32[16,1,128]{2,1,0:T(1,128)S(1)}, u32[]{:S(2)}) copy-start(f32[16,1,128]{2,1,0:T(1,128)S(1)} %convert_element_type.210) | copy-start | bytes 24580
  508.7 473.6 %all-to-all-start = ((bf16[32,160,2048]{2,1,0:T(8,128)(2,1)}), bf16[32,160,2048]{2,1,0:T(8,128)(2,1)}, u32[]{:S(2)}, u32[]{:S(2)}) async-start(bf16[32,160,2048]{2,1,0:T(8,128)(2,1)} %bitcast.277), calls=%async_computation | async-start | bytes 41943040 | tf_op jit(solution)/shard_map/all_to_all | solution.py:61
  982.3 477.5 %all-to-all-start.2 = ((bf16[32,160,2048]{2,1,0:T(8,128)(2,1)}), bf16[32,160,2048]{2,1,0:T(8,128)(2,1)}, u32[]{:S(2)}, u32[]{:S(2)}) async-start(bf16[32,160,2048]{2,1,0:T(8,128)(2,1)} %fusion), calls=%async_computation.2 | async-start | bytes 41943040 | tf_op jit(solution)/shard_map/all_to_all | solution.py:61
  1546.3 477.5 %all-to-all-start.3 = ((bf16[32,160,2048]{2,1,0:T(8,128)(2,1)}), bf16[32,160,2048]{2,1,0:T(8,128)(2,1)}, u32[]{:S(2)}, u32[]{:S(2)}) async-start(bf16[32,160,2048]{2,1,0:T(8,128)(2,1)} %bitcast.276), calls=%async_computation.3 | async-start | bytes 41943040 | tf_op jit(solution)/shard_map/all_to_all | solution.py:67
  2023.7 485.6 %all-to-all-start.1 = ((bf16[32,160,2048]{2,1,0:T(8,128)(2,1)}), bf16[32,160,2048]{2,1,0:T(8,128)(2,1)}, u32[]{:S(2)}, u32[]{:S(2)}) async-start(bf16[32,160,2048]{2,1,0:T(8,128)(2,1)} %bitcast.275), calls=%async_computation.1 | async-start | bytes 41943040 | tf_op jit(solution)/shard_map/all_to_all | solution.py:67
  2033.6 533.6 %all-reduce.18.cloned.1.call-start = ((), (), s32[]{:S(2)}) async-start(), calls=%async_computation.13 | async-start | bytes 8388608 | tf_op jit(solution)/shard_map/psum | solution.py:231
  2090.0 682.1 %all-reduce.20.cloned.1.call-start = ((), (), s32[]{:S(2)}) async-start(), calls=%async_computation.18 | async-start | bytes 8388608 | tf_op jit(solution)/shard_map/psum | solution.py:185
  2509.3 41.3 %copy-start.25 = (f32[512,8]{1,0:T(8,128)S(1)}, f32[512,8]{1,0:T(8,128)}, u32[]{:S(2)}) copy-start(f32[512,8]{1,0:T(8,128)} %copy-done.24) | copy-start | bytes 49156
  2680.3 170.5 %reduce-scatter.7.cloned.1.call-start = ((), (), s32[]{:S(2)}) async-start(), calls=%async_computation.15 | async-start | bytes 2228224 | tf_op jit(solution)/shard_map/reduce_scatter | solution.py:311
  2684.3 183.2 %reduce-scatter.9.cloned.1.call-start = ((), (), s32[]{:S(2)}) async-start(), calls=%async_computation.16 | async-start | bytes 2228224 | tf_op jit(solution)/shard_map/reduce_scatter | solution.py:312
  2686.7 542.5 %reduce-scatter.11.cloned.1.call-start = ((), (), s32[]{:S(2)}) async-start(), calls=%async_computation.17 | async-start | bytes 17825792 | tf_op jit(solution)/shard_map/reduce_scatter | solution.py:313
  2700.7 883.5 %reduce-scatter.5.cloned.1.call-start = ((), (), s32[]{:S(2)}) async-start(), calls=%async_computation.14 | async-start | bytes 17825792 | tf_op jit(solution)/shard_map/reduce_scatter | solution.py:310
  2842.5 741.8 %copy-start.1 = (bf16[2,384,2048]{2,1,0:T(8,128)(2,1)S(1)}, bf16[2,384,2048]{2,1,0:T(8,128)(2,1)}, u32[]{:S(2)}) copy-start(bf16[2,384,2048]{2,1,0:T(8,128)(2,1)} %param.27) | copy-start | bytes 9437188
  (58 other events, 347.8 us)
Sparse Core Ops, SparseCore 0:
  10.8 55.4 all-gather.8
  69.0 53.9 all-gather.6
  125.8 110.9 all-gather.10
  239.4 110.4 all-gather.12
  360.7 27.6 all-reduce.15
  2090.1 29.2 all-reduce.17
  2680.5 30.4 all-reduce.19
  2713.8 72.6 reduce-scatter.6
  2789.4 78.0 reduce-scatter.8
  2870.2 359.0 reduce-scatter.10
  3232.1 352.0 reduce-scatter.4
where the time goes:
time: 3600 us; the launch traced here: 3590 us
  waiting for transfers between devices  2590 us (72%)
  local copies, waits for them, and re-layouts  333 us (9%)
  matrix products  285 us (8%)
  blocking collectives  175 us (5%)
  other arithmetic  152 us (4%)
  starting transfers between devices  40.8 us (1%)
    all_to_all x2, waiting for transfers between devices, to_sources(): lax.all_to_all(expert_rows, 'expert', split_axis=0, concat_axis=0, tiled=...  851 us
    all_to_all x2, waiting for transfers between devices, to_owners(): lax.all_to_all(picked, 'expert', split_axis=0, concat_axis=0, tiled=True)  802 us
    reduce_scatter x1, waiting for transfers between devices, local(): lax.psum_scatter(grad_output_w, 'expert', scatter_dimension=0, tiled=True)  362 us
    reduce_scatter x1, waiting for transfers between devices, local(): lax.psum_scatter(grad_query_w, 'expert', scatter_dimension=0, tiled=True)  355 us
    all_gather x1, waiting for transfers between devices, local(): lax.all_gather(query_weight, 'expert', axis=0, tiled=True)  110 us
    unnamed x2, blocking collectives  96.2 us
    gather x2, local copies, waits for them, and re-layouts, to_sources(): return returned.reshape(-1, width)[places_sent].astype(jnp.float32)  82.2 us
  transfers between devices with their start and end apart: 15, of which 10 were waited for; matrix products, arithmetic and copies ran while one was open for 14% of the time, Pallas kernels for 0%

commit v1 on v0

--- a/solution.py
+++ b/solution.py
@@ -1,6 +1,9 @@
+import functools
 import jax
 import jax.numpy as jnp
 from jax import lax
+from jax.experimental import pallas as pl
+from jax.experimental.pallas import tpu as pltpu
 from jax.sharding import PartitionSpec as P
 
 HEAD_SIZE = 128
@@ -334,9 +337,497 @@
     )
 
 
+MESH = pl.DeviceIdType.MESH
+ZS, YS, XS = 4, 2, 2
+
+def place():
+    e = lax.axis_index("expert"); c = lax.axis_index("tensor")
+    return e // 4, (e // 2) % 2, e % 2, c
+
+def ident(z, y, x, c):
+    return (z * 4 + y * 2 + x, c)
+
+def greet(share):
+    z, y, x, c = place()
+    bar = pltpu.get_barrier_semaphore()
+    def hello(dev):
+        pl.semaphore_signal(bar, inc=1, device_id=dev, device_id_type=MESH)
+    hello(ident(z, y, 1 - x, c))
+    hello(ident(z, 1 - y, x, c))
+    n = 2
+    if share:
+        hello(ident(z, y, x, 1 - c)); n = 3
+    pl.when(z > 0)(lambda: hello(ident(z - 1, y, x, c)))
+    pl.when(z < ZS - 1)(lambda: hello(ident(z + 1, y, x, c)))
+    pl.semaphore_wait(bar, n + (z > 0).astype(jnp.int32) + (z < ZS - 1).astype(jnp.int32))
+
+def gather_kernel(n, share, *refs):
+    ins, outs = refs[:n], refs[n:2 * n]
+    stage = refs[2 * n:3 * n]
+    ss, rs, ls = refs[3 * n:]
+    z, y, x, c = place()
+    greet(share)
+    rows = [(r.shape[0] // 2 if share else r.shape[0]) for r in ins]
+    full = [r.shape[0] for r in ins]
+    def start(a, b, part):
+        base = (z * 0 + b) * full[a]
+        if share:
+            base = base + c * rows[a]
+        half = rows[a] // 2
+        if part == "w":
+            return pl.ds(pl.multiple_of(base, 16), rows[a])
+        return pl.ds(pl.multiple_of(base + (0 if part == "p" else half), 16), half)
+    def src_own(a, part):
+        half = rows[a] // 2
+        base = c * rows[a] if share else 0
+        if part == "w":
+            return ins[a].at[pl.ds(base, rows[a]), :]
+        off = 0 if part == "p" else half
+        return ins[a].at[pl.ds(base + off, half), :]
+    keys = {}
+    def num(k):
+        return keys.setdefault(k, len(keys))
+    def cp(k, a, b, part, dev, own=False):
+        i = num(k)
+        dst = outs[a].at[start(a, b, part), :]
+        src = src_own(a, part) if own else dst
+        return pltpu.make_async_remote_copy(src_ref=src, dst_ref=dst, send_sem=ss.at[i, a], recv_sem=rs.at[i, a],
+                                            device_id=dev, device_id_type=MESH)
+    def each(f):
+        for a in range(n):
+            f(a)
+    xn, yn, zu, zd, sib = ident(z, y, 1 - x, c), ident(z, 1 - y, x, c), ident(z + 1, y, x, c), ident(z - 1, y, x, c), ident(z, y, x, 1 - c)
+    def bid(s, yy, xx):
+        return s * 4 + yy * 2 + xx
+    sends = []
+    me = bid(z, y, x)
+    locs = []
+    def own_in(a):
+        return pltpu.make_async_copy(ins[a], stage[a], ls.at[a, 0])
+    def own_out(a):
+        return pltpu.make_async_copy(stage[a], outs[a].at[pl.ds(pl.multiple_of(me * full[a], 16), full[a]), :], ls.at[a, 1])
+    def send(cond, k, b, part, dev, own=False):
+        def go():
+            each(lambda a: cp(k, a, b, part, dev, own).start())
+        if cond is None: go()
+        else: pl.when(cond)(go)
+        sends.append((cond, k, b, part, dev, own))
+    def recv(cond, k, b, part, dev):
+        def go():
+            each(lambda a: cp(k, a, b, part, dev).wait_recv())
+        if cond is None: go()
+        else: pl.when(cond)(go)
+    send(z < 3, ("u", 0), me, "w", zu, True)
+    send(z > 0, ("d", 0), me, "w", zd, True)
+    slots = [(0, 0)] + [(d, sg) for d in (1, 2, 3) for sg in (-1, 1)]
+    def cond_of(d, sg):
+        if d == 0: return None
+        return (z - d >= 0) if sg < 0 else (z + d <= 3)
+    def A(d, sg):
+        s = z + sg * d; cnd = cond_of(d, sg); own = d == 0
+        b = bid(s, y, x)
+        send(cnd, ("xP", d, sg), b, "p", xn, own)
+        send(cnd, ("yQ", d, sg), b, "q", yn, own)
+        send(cnd, ("xQ", d, sg), b, "q", xn, own)
+        send(cnd, ("yP", d, sg), b, "p", yn, own)
+        if share and not own:
+            send(cnd, ("s0", d, sg), b, "w", sib)
+    def B(d, sg):
+        s = z + sg * d; cnd = cond_of(d, sg)
+        recv(cnd, ("xP", d, sg), bid(s, y, 1 - x), "p", xn)
+        send(cnd, ("yPr", d, sg), bid(s, y, 1 - x), "p", yn)
+        recv(cnd, ("yQ", d, sg), bid(s, 1 - y, x), "q", yn)
+        send(cnd, ("xQr", d, sg), bid(s, 1 - y, x), "q", xn)
+    def C(d, sg):
+        s = z + sg * d; cnd = cond_of(d, sg)
+        recv(cnd, ("xQ", d, sg), bid(s, y, 1 - x), "q", xn)
+        if share: send(cnd, ("s1", d, sg), bid(s, y, 1 - x), "w", sib)
+        recv(cnd, ("yP", d, sg), bid(s, 1 - y, x), "p", yn)
+        if share: send(cnd, ("s2", d, sg), bid(s, 1 - y, x), "w", sib)
+        recv(cnd, ("yPr", d, sg), bid(s, 1 - y, 1 - x), "p", yn)
+        recv(cnd, ("xQr", d, sg), bid(s, 1 - y, 1 - x), "q", xn)
+        if share: send(cnd, ("s3", d, sg), bid(s, 1 - y, 1 - x), "w", sib)
+    A(0, 0)
+    each(lambda a: own_in(a).start())
+    each(lambda a: own_in(a).wait())
+    each(lambda a: own_out(a).start())
+    B(0, 0)
+    prev = [(0, 0)]
+    for d in (1, 2, 3):
+        recv(z - d >= 0, ("u", d - 1), bid(z - d, y, x), "w", zd)
+        if d < 3:
+            send((z - d >= 0) & (z < 3), ("u", d), bid(z - d, y, x), "w", zu)
+        A(d, -1)
+        recv(z + d <= 3, ("d", d - 1), bid(z + d, y, x), "w", zu)
+        if d < 3:
+            send((z + d <= 3) & (z > 0), ("d", d), bid(z + d, y, x), "w", zd)
+        A(d, 1)
+        B(d, -1); B(d, 1)
+        for p in prev: C(*p)
+        prev = [(d, -1), (d, 1)]
+    for p in prev: C(*p)
+    each(lambda a: own_out(a).wait())
+    if share:
+        for d, sg in slots:
+            s = z + sg * d; cnd = cond_of(d, sg)
+            def sibwait(k, b):
+                def go():
+                    for a in range(n):
+                        i = num(k)
+                        r = outs[a].at[pl.ds(pl.multiple_of(b * full[a] + (1 - c) * rows[a], 16), rows[a]), :]
+                        pltpu.make_async_remote_copy(src_ref=r, dst_ref=r, send_sem=ss.at[i, a], recv_sem=rs.at[i, a], device_id=sib, device_id_type=MESH).wait_recv()
+                if cnd is None: go()
+                else: pl.when(cnd)(go)
+            if d: sibwait(("s0", d, sg), bid(s, y, x))
+            sibwait(("s1", d, sg), bid(s, y, 1 - x))
+            sibwait(("s2", d, sg), bid(s, 1 - y, x))
+            sibwait(("s3", d, sg), bid(s, 1 - y, 1 - x))
+    for cond, k, b, part, dev, own in sends:
+        def go():
+            each(lambda a: cp(k, a, b, part, dev, own).wait_send())
+        if cond is None: go()
+        else: pl.when(cond)(go)
+    assert len(keys) <= NKEYS, len(keys)
+
+NKEYS = 80
+def all_gather_blocks(arrays, cid, share=False):
+    n = len(arrays)
+    anyspec = pl.BlockSpec(memory_space=pltpu.HBM)
+    return pl.pallas_call(
+        functools.partial(gather_kernel, n, share),
+        out_shape=[jax.ShapeDtypeStruct((16 * a.shape[0], a.shape[1]), a.dtype) for a in arrays],
+        in_specs=[anyspec] * n, out_specs=[anyspec] * n,
+        scratch_shapes=[pltpu.VMEM(a.shape, a.dtype) for a in arrays] + [
+            pltpu.SemaphoreType.DMA((NKEYS, n)), pltpu.SemaphoreType.DMA((NKEYS, n)), pltpu.SemaphoreType.DMA((n, 2))],
+        compiler_params=pltpu.CompilerParams(collective_id=cid, has_side_effects=True),
+        name="gather_blocks",
+    )(*arrays)
+
+
+SLOTS = [(3, -1), (3, 1), (2, -1), (2, 1), (1, -1), (1, 1), (0, 0)]
+CH = 32
+
+def scatter_kernel(part, out, A, SR, RP, RP2, RQ, RQ2, ZU, ZD, ls, ss, rs):
+    z, y, x, c = place()
+    rows = A.shape[1]; half = rows // 2
+    greet(True)
+    xn, yn, zu, zd, sib = ident(z, y, 1 - x, c), ident(z, 1 - y, x, c), ident(z + 1, y, x, c), ident(z - 1, y, x, c), ident(z, y, x, 1 - c)
+    keys = {}
+    def num(k): return keys.setdefault(k, len(keys))
+    def cond_of(d, sg):
+        if d == 0: return None
+        return (z - d >= 0) if sg < 0 else (z + d <= 3)
+    def guard(cnd, go):
+        if cnd is None: go()
+        else: pl.when(cnd)(go)
+    sent = []
+    def rc(k, src, dst, dev):
+        i = num(k)
+        return pltpu.make_async_remote_copy(src_ref=src, dst_ref=dst, send_sem=ss.at[i], recv_sem=rs.at[i], device_id=dev, device_id_type=MESH)
+    def send(cnd, k, src, dst, dev):
+        guard(cnd, lambda: rc(k, src, dst, dev).start())
+        sent.append((cnd, k, src, dst, dev))
+    def recv(cnd, k, dst, dev):
+        guard(cnd, lambda: rc(k, dst, dst, dev).wait_recv())
+    def blocks(s):
+        b = s * 4
+        return b + y * 2 + x, b + y * 2 + 1 - x, b + (1 - y) * 2 + x, b + (1 - y) * 2 + 1 - x
+    Ph, Qh = pl.ds(0, half), pl.ds(half, half)
+    def part_at(b, cc):
+        return part.at[pl.ds(pl.multiple_of(b * 2 * rows + cc * rows, 16), rows), :]
+    def load(b):
+        return pltpu.make_async_copy(part_at(b, c), A.at[b], ls.at[b])
+    for d, sg in SLOTS:
+        cnd = cond_of(d, sg); s = z + sg * d
+        for q, b in enumerate(blocks(s)):
+            guard(cnd, lambda: load(b).start())
+            send(cnd, ("sib", d, sg, q), part_at(b, 1 - c), SR.at[b], sib)
+    def sum_into(dst, row0, terms, n=half):
+        def step(i, _):
+            r = pl.ds(row0 + i * CH, CH)
+            acc = dst[r, :].astype(jnp.float32)
+            for t, off in terms:
+                acc = acc + t[pl.ds(off + i * CH, CH), :].astype(jnp.float32)
+            dst[r, :] = acc.astype(dst.dtype)
+            return 0
+        lax.fori_loop(0, n // CH, step, 0)
+    def S1(i):
+        d, sg = SLOTS[i]; cnd = cond_of(d, sg); s = z + sg * d
+        m, xx, yy, dd = blocks(s)
+        def go():
+            for q, b in enumerate((m, xx, yy, dd)):
+                load(b).wait()
+                rc(("sib", d, sg, q), SR.at[b], SR.at[b], sib).wait_recv()
+            sum_into(A.at[dd], 0, [(SR.at[dd], 0)], rows)
+        guard(cnd, go)
+        send(cnd, ("yd", i), A.at[dd, Ph, :], RP.at[s, 1], yn)
+        send(cnd, ("xd", i), A.at[dd, Qh, :], RQ.at[s, 1], xn)
+        guard(cnd, lambda: (sum_into(A.at[yy], 0, [(SR.at[yy], 0)]), sum_into(A.at[xx], half, [(SR.at[xx], half)]))and None)
+        send(cnd, ("yy", i), A.at[yy, Ph, :], RP.at[s, 0], yn)
+        send(cnd, ("xx", i), A.at[xx, Qh, :], RQ.at[s, 0], xn)
+    def S2(i):
+        d, sg = SLOTS[i]; cnd = cond_of(d, sg); s = z + sg * d
+        m, xx, yy, dd = blocks(s)
+        recv(cnd, ("yd", i), RP.at[s, 1], yn)
+        guard(cnd, lambda: sum_into(A.at[xx], 0, [(SR.at[xx], 0), (RP.at[s, 1], 0)]))
+        send(cnd, ("x2", i), A.at[xx, Ph, :], RP2.at[s], xn)
+        recv(cnd, ("xd", i), RQ.at[s, 1], xn)
+        guard(cnd, lambda: sum_into(A.at[yy], half, [(SR.at[yy], half), (RQ.at[s, 1], 0)]))
+        send(cnd, ("y2", i), A.at[yy, Qh, :], RQ2.at[s], yn)
+    def S3(i):
+        d, sg = SLOTS[i]; cnd = cond_of(d, sg); s = z + sg * d
+        m = blocks(s)[0]
+        recv(cnd, ("yy", i), RP.at[s, 0], yn)
+        recv(cnd, ("xx", i), RQ.at[s, 0], xn)
+        recv(cnd, ("x2", i), RP2.at[s], xn)
+        recv(cnd, ("y2", i), RQ2.at[s], yn)
+        base_p = [(SR.at[m], 0), (RP.at[s, 0], 0), (RP2.at[s], 0)]
+        base_q = [(SR.at[m], half), (RQ.at[s, 0], 0), (RQ2.at[s], 0)]
+        if d:
+            back = (z > 0) if sg > 0 else (z < 3)
+            Z = ZU if sg > 0 else ZD
+            name = "u" if sg > 0 else "d"
+            dn, up = (zd, zu) if sg > 0 else (zu, zd)
+            has = d <= 2
+            def plain():
+                sum_into(A.at[m], 0, base_p); sum_into(A.at[m], half, base_q)
+            if has:
+                recv(cnd & back, (name, d), Z.at[d], dn)
+                pl.when(cnd & back)(lambda: (sum_into(A.at[m], 0, base_p + [(Z.at[d], 0)]), sum_into(A.at[m], half, base_q + [(Z.at[d], half)])) and None)
+                pl.when(cnd & jnp.logical_not(back))(plain)
+            else:
+                pl.when(cnd)(plain)
+            send(cnd, (name, d - 1), A.at[m], Z.at[d - 1], up)
+        else:
+            recv(z > 0, ("u", 0), ZU.at[0], zd)
+            recv(z < 3, ("d", 0), ZD.at[0], zu)
+            lo = jnp.where(z > 0, 1.0, 0.0); hi = jnp.where(z < 3, 1.0, 0.0)
+            def emit(row0, terms, flags):
+                def step(i, _):
+                    acc = A[m, pl.ds(row0 + i * CH, CH), :].astype(jnp.float32)
+                    for t, off in terms:
+                        acc = acc + t[pl.ds(off + i * CH, CH), :].astype(jnp.float32)
+                    if flags[0]: acc = acc + ZU[0, pl.ds(row0 + i * CH, CH), :].astype(jnp.float32)
+                    if flags[1]: acc = acc + ZD[0, pl.ds(row0 + i * CH, CH), :].astype(jnp.float32)
+                    out[pl.ds(pl.multiple_of(c * rows + row0 + i * CH, CH), CH), :] = acc
+                    return 0
+                lax.fori_loop(0, half // CH, step, 0)
+            for cc, fl in ((z == 0, (False, True)), (z == 3, (True, False)), ((z > 0) & (z < 3), (True, True))):
+                @pl.when(cc)
+                def _(fl=fl):
+                    emit(0, base_p, fl); emit(half, base_q, fl)
+            mine = out.at[pl.ds(pl.multiple_of(c * rows, 16), rows), :]
+            other = out.at[pl.ds(pl.multiple_of((1 - c) * rows, 16), rows), :]
+            send(None, ("fin",), mine, mine, sib)
+            recv(None, ("fin",), other, sib)
+    n = len(SLOTS)
+    for i in range(n + 2):
+        if i < n: S1(i)
+        if 0 <= i - 1 < n: S2(i - 1)
+        if 0 <= i - 2 < n: S3(i - 2)
+    for cnd, k, src, dst, dev in sent:
+        guard(cnd, lambda: rc(k, src, dst, dev).wait_send())
+    assert len(keys) <= NK, len(keys)
+
+NK = 90
+def reduce_scatter_rows(part, cid):
+    total, width = part.shape
+    rows = total // 32
+    half = rows // 2
+    bf = part.dtype
+    return pl.pallas_call(
+        scatter_kernel,
+        out_shape=jax.ShapeDtypeStruct((2 * rows, width), jnp.float32),
+        in_specs=[pl.BlockSpec(memory_space=pltpu.HBM)], out_specs=pl.BlockSpec(memory_space=pltpu.VMEM),
+        scratch_shapes=[
+            pltpu.VMEM((16, rows, width), bf), pltpu.VMEM((16, rows, width), bf),
+            pltpu.VMEM((4, 2, half, width), bf), pltpu.VMEM((4, half, width), bf),
+            pltpu.VMEM((4, 2, half, width), bf), pltpu.VMEM((4, half, width), bf),
+            pltpu.VMEM((3, rows, width), bf), pltpu.VMEM((3, rows, width), bf),
+            pltpu.SemaphoreType.DMA((16,)), pltpu.SemaphoreType.DMA((NK,)), pltpu.SemaphoreType.DMA((NK,))],
+        compiler_params=pltpu.CompilerParams(collective_id=cid, has_side_effects=True, vmem_limit_bytes=67043328),
+        name="scatter_rows",
+    )(part)
+
+def tables(routes_all, weights_all, first, local_experts, capacity):
+    n, rows, top = routes_all.shape
+    tri = (jnp.arange(rows)[:, None] <= jnp.arange(rows)[None, :]).astype(jnp.bfloat16)
+    picks, scale, token_w = [], [], []
+    for l in range(local_experts):
+        hit = routes_all == (first + l)
+        member = jnp.any(hit, axis=-1)
+        weight = jnp.sum(jnp.where(hit, weights_all, 0.0), axis=-1)
+        rank = jnp.dot(member.astype(jnp.bfloat16), tri, preferred_element_type=jnp.float32).astype(jnp.int32)
+        slot = jnp.where(member, rank - 1, -1)
+        pick = slot[:, None, :] == jnp.arange(capacity, dtype=jnp.int32)[None, :, None]
+        picks.append(pick)
+        scale.append(jnp.sum(jnp.where(pick, weight[:, None, :], 0.0), axis=-1, keepdims=True))
+    return picks, scale
+
+
+def local_block(
+    tokens, attn_gain, moe_gain, query_gain, key_gain, query_weight, key_weight, value_matrix, output_weight,
+    gate_proj, up_proj, down_proj, gate_weights, routes, doc_start, cotangent,
+):
+    f32, bf16 = jnp.float32, jnp.bfloat16
+    tok_rows, width = tokens.shape
+    top_count = routes.shape[1]
+    n_chips = ZS * YS * XS
+    assigned = tok_rows * top_count
+    lanes = 128
+    list_rows = assigned // lanes
+    small = jnp.concatenate(
+        [
+            attn_gain.astype(f32).reshape(-1, lanes), moe_gain.astype(f32).reshape(-1, lanes),
+            jnp.pad(jnp.concatenate([query_gain, key_gain]).astype(f32), (0, lanes - 2 * query_gain.shape[0])).reshape(1, lanes),
+            routes.astype(f32).reshape(list_rows, lanes), gate_weights.reshape(list_rows, lanes),
+        ], axis=0)
+    gain_rows = attn_gain.shape[0] // lanes
+    small = jnp.pad(small, ((0, -small.shape[0] % 32), (0, 0)))
+    full_query, full_key, full_value, full_output, gathered = all_gather_blocks(
+        [query_weight, key_weight, value_matrix, output_weight, small], 1)
+    (dy_all,) = all_gather_blocks([cotangent], 2, share=True)
+    gathered = gathered.reshape(n_chips, -1, lanes)
+    gain_attn = gathered[:, :gain_rows].reshape(-1)
+    gain_moe = gathered[:, gain_rows:2 * gain_rows].reshape(-1)
+    per = query_gain.shape[0]
+    gain_query = gathered[:, 2 * gain_rows, :per].reshape(-1)
+    gain_key = gathered[:, 2 * gain_rows, per:2 * per].reshape(-1)
+    off = 2 * gain_rows + 1
+    routes_all = gathered[:, off:off + list_rows].astype(jnp.int32).reshape(n_chips, tok_rows, top_count)
+    weights_all = gathered[:, off + list_rows:off + 2 * list_rows].reshape(n_chips, tok_rows, top_count)
+
+    cos_table, sin_table, allowed = doc_tables(doc_start)
+    heads_here = full_query.shape[1] // HEAD_SIZE
+    kv_here = full_key.shape[1] // HEAD_SIZE
+    query_group_width = heads_here // kv_here
+    inputs = tokens.astype(f32)
+    unit_attn, factor_attn = rms_parts(inputs)
+    normalized_input = (unit_attn * gain_attn).astype(bf16)
+    query_raw = jnp.dot(normalized_input, full_query, preferred_element_type=f32).reshape(tok_rows, heads_here, HEAD_SIZE)
+    key_unrotated = jnp.dot(normalized_input, full_key, preferred_element_type=f32).reshape(tok_rows, kv_here, HEAD_SIZE)
+    values_low = jnp.dot(normalized_input, full_value, preferred_element_type=f32).astype(bf16).reshape(tok_rows, kv_here, HEAD_SIZE)
+    query_unit, query_factor = rms_parts(query_raw)
+    key_unit, key_factor = rms_parts(key_unrotated)
+    queries_low = rotate(query_unit * gain_query, cos_table, sin_table).astype(bf16)
+    keys_low = rotate(key_unit * gain_key, cos_table, sin_table).astype(bf16)
+    grouped_heads = queries_low.reshape(tok_rows, kv_here, query_group_width, HEAD_SIZE)
+    scores = scores_of(grouped_heads, keys_low, allowed)
+    row_peak = jnp.max(scores, axis=-1, keepdims=True)
+    weights = jnp.exp(scores - row_peak)
+    totals = jnp.sum(weights, axis=-1, keepdims=True)
+    probs_low = (weights / totals).astype(bf16)
+    log_total = row_peak + jnp.log(totals)
+    mixed_low = (
+        jnp.einsum("ngqk,knd->qngd", probs_low, values_low, preferred_element_type=f32)
+        .reshape(tok_rows, heads_here * HEAD_SIZE).astype(bf16))
+    attn_part = jnp.einsum("th,dh->td", mixed_low, full_output, preferred_element_type=f32)
+    hidden = inputs + lax.psum(attn_part, "tensor")
+    unit_moe, factor_moe = rms_parts(hidden)
+    normed_moe = (unit_moe * gain_moe).astype(bf16)
+
+    local_experts = gate_proj.shape[0]
+    experts = n_chips * local_experts
+    capacity = assigned * 5 // (4 * experts)
+    chip = lax.axis_index("expert")
+    picks, scale = tables(routes_all, weights_all, chip * local_experts, local_experts, capacity)
+    (x_all,) = all_gather_blocks([normed_moe], 3, share=True)
+    x_all = x_all.reshape(n_chips, tok_rows, width)
+    dy_all = dy_all.reshape(n_chips, tok_rows, width)
+    y_rows, dx_rows, gates_tok, grads = [], [], [], []
+    for l in range(local_experts):
+        pick = picks[l].astype(bf16)
+        def take(source):
+            return jnp.einsum("sjt,std->sjd", pick, source, preferred_element_type=f32)
+        w_slot = scale[l].reshape(-1, 1)
+        xs = take(x_all).astype(bf16).reshape(-1, width)
+        dys = (scale[l] * take(dy_all)).astype(bf16).reshape(-1, width)
+        gate_value = jnp.dot(xs, gate_proj[l], preferred_element_type=f32)
+        up_value = jnp.dot(xs, up_proj[l], preferred_element_type=f32)
+        sigmoid_gate = jax.nn.sigmoid(gate_value)
+        act = (gate_value * sigmoid_gate * up_value).astype(bf16)
+        y_rows.append((w_slot * jnp.dot(act, down_proj[l], preferred_element_type=f32)).astype(bf16))
+        grad_act = jnp.einsum("rd,fd->rf", dys, down_proj[l], preferred_element_type=f32)
+        gates_slot = jnp.sum(act.astype(f32) * grad_act, axis=-1, keepdims=True) / jnp.where(w_slot > 0, w_slot, 1.0)
+        gates_tok.append(jnp.sum(jnp.where(picks[l], gates_slot.reshape(n_chips, capacity, 1), 0.0), axis=1))
+        up_low = (grad_act * gate_value * sigmoid_gate).astype(bf16)
+        gate_low = (grad_act * up_value * sigmoid_gate * (1.0 + gate_value * (1.0 - sigmoid_gate))).astype(bf16)
+        dx = jnp.einsum("rf,df->rd", gate_low, gate_proj[l], preferred_element_type=f32)
+        dx = dx + jnp.einsum("rf,df->rd", up_low, up_proj[l], preferred_element_type=f32)
+        dx_rows.append(dx.astype(bf16))
+        grads.append((
+            jnp.einsum("rd,rf->df", xs, gate_low, preferred_element_type=f32),
+            jnp.einsum("rd,rf->df", xs, up_low, preferred_element_type=f32),
+            jnp.einsum("rf,rd->fd", act, dys, preferred_element_type=f32)))
+    pick_both = jnp.concatenate(picks, axis=1).astype(bf16)
+    def put(rows):
+        both = jnp.concatenate([r.reshape(n_chips, capacity, width) for r in rows], axis=1)
+        return jnp.einsum("sjt,sjd->std", pick_both, both, preferred_element_type=f32).astype(bf16).reshape(-1, width)
+    grad_normed_moe = reduce_scatter_rows(put(dx_rows), 4)
+    moe_out = reduce_scatter_rows(put(y_rows), 5)
+    grad_gate_w, grad_up_w, grad_down = (jnp.stack([g[i] for g in grads]) for i in range(3))
+    block_out = (hidden + moe_out).astype(bf16)
+    gates_back = lax.all_to_all(jnp.stack(gates_tok, axis=1), "expert", split_axis=0, concat_axis=0, tiled=True)
+    gates_back = lax.psum(gates_back, "tensor").reshape(experts, tok_rows)
+    grad_gates = jnp.sum(
+        jnp.where(routes[:, :, None] == jnp.arange(experts, dtype=jnp.int32), gates_back.T[:, None, :], 0.0), axis=-1)
+
+    upstream = cotangent.astype(f32)
+    grad_moe_gain = jnp.sum(grad_normed_moe * unit_moe, axis=0)
+    grad_hidden = upstream + norm_back(grad_normed_moe * gain_moe, unit_moe, factor_moe)
+    grad_attn_low = grad_hidden.astype(bf16)
+    grad_mixed = jnp.einsum("td,dh->th", grad_attn_low, full_output, preferred_element_type=f32)
+    grad_mixed_low = grad_mixed.astype(bf16).reshape(tok_rows, kv_here, query_group_width, HEAD_SIZE)
+    grad_output_w = jnp.einsum("td,th->dh", grad_attn_low, mixed_low, preferred_element_type=f32)
+    scores = scores_of(grouped_heads, keys_low, allowed)
+    prob_full = jnp.exp(scores - log_total)
+    grad_probs = jnp.einsum("qngd,knd->ngqk", grad_mixed_low, values_low, preferred_element_type=f32)
+    grad_values = jnp.einsum(
+        "ngqk,qngd->knd", prob_full.astype(bf16), grad_mixed_low, preferred_element_type=f32).astype(bf16)
+    row_delta = jnp.sum(prob_full * grad_probs, axis=-1, keepdims=True)
+    grad_scores = (prob_full * (grad_probs - row_delta)).astype(bf16)
+    score_scale = HEAD_SIZE ** (-0.5)
+    grad_queries = (
+        jnp.einsum("ngqk,knd->qngd", grad_scores, keys_low, preferred_element_type=f32)
+        .reshape(tok_rows, heads_here, HEAD_SIZE) * score_scale)
+    grad_keys = jnp.einsum("ngqk,qngd->knd", grad_scores, grouped_heads, preferred_element_type=f32) * score_scale
+    grad_qhead = rotate(grad_queries, cos_table, -sin_table)
+    grad_khead = rotate(grad_keys, cos_table, -sin_table)
+    query_gain_part = jnp.sum(grad_qhead * query_unit, axis=(0, 1))
+    key_gain_part = jnp.sum(grad_khead * key_unit, axis=(0, 1))
+    grad_query_low = norm_back(grad_qhead * gain_query, query_unit, query_factor).astype(bf16).reshape(tok_rows, -1)
+    grad_key_low = norm_back(grad_khead * gain_key, key_unit, key_factor).astype(bf16).reshape(tok_rows, -1)
+    grad_value_low = grad_values.reshape(tok_rows, -1)
+    grad_normed_part = jnp.einsum("th,dh->td", grad_query_low, full_query, preferred_element_type=f32)
+    grad_normed_part = grad_normed_part + jnp.einsum("th,dh->td", grad_key_low, full_key, preferred_element_type=f32)
+    grad_normed_part = grad_normed_part + jnp.einsum("th,dh->td", grad_value_low, full_value, preferred_element_type=f32)
+    grad_normed = lax.psum(grad_normed_part.astype(bf16), "tensor").astype(f32)
+    grad_attn_gain_part = jnp.sum(grad_normed * unit_attn, axis=0)
+    grad_tokens = grad_hidden + norm_back(grad_normed * gain_attn, unit_attn, factor_attn)
+
+    grad_query_w = jnp.einsum("td,th->dh", normalized_input, grad_query_low, preferred_element_type=f32)
+    grad_key_w = jnp.einsum("td,th->dh", normalized_input, grad_key_low, preferred_element_type=f32)
+    grad_value_w = jnp.einsum("td,th->dh", normalized_input, grad_value_low, preferred_element_type=f32)
+    shares = tuple(
+        lax.psum_scatter(v, "expert", scatter_dimension=0, tiled=True)
+        for v in (grad_query_w, grad_key_w, grad_value_w, grad_output_w))
+    gains = jnp.concatenate([grad_attn_gain_part, grad_moe_gain, query_gain_part, key_gain_part])
+    head_gains = lax.psum(gains[2 * width:], ("expert", "tensor"))
+    model_gains = lax.psum(gains[:2 * width], "expert")
+    def own(v):
+        size = v.shape[0] // n_chips
+        return lax.dynamic_slice_in_dim(v, chip * size, size, 0)
+    return (
+        block_out, grad_tokens, *shares,
+        own(model_gains[:width]), own(model_gains[width:]), own(head_gains[:HEAD_SIZE]), own(head_gains[HEAD_SIZE:]),
+        grad_gate_w, grad_up_w, grad_down, grad_gates,
+    )
+
+
 def solution(mesh):
+    wide = mesh.shape["expert"] == ZS * YS * XS and mesh.shape["tensor"] == 2
     return jax.shard_map(
-        local,
+        local_block if wide else local,
         mesh=mesh,
         in_specs=(
             P("expert", None),

time: 3600 us -> 2200 us (0.61)
  waiting for transfers between devices: 2590 us -> 712 us
  Pallas kernels: 0 us -> 788 us
  local copies, waits for them, and re-layouts: 333 us -> 57.7 us
  matrix products: 285 us -> 401 us
  blocking collectives: 175 us -> 105 us
  other arithmetic: 152 us -> 103 us
    all_to_all x4 -> x1, waiting for transfers between devices: 1650 us -> 0.01 us  [local_block(): lax.all_to_all(jnp.stack(gates_tok, axis=1), 'expert', split_axis=0, conc...]
    pallas_call x0 -> x5, Pallas kernels: none -> 788 us  [the longest x3 454 us: all_gather_blocks(): pl.pallas_call(functools.partial(gather_kernel, n, share), out_shape=[jax...]
    gather x6 -> x0, local copies, waits for them, and re-layouts: 221 us -> none  [the longest x2 82.2 us: to_sources(): return returned.reshape(-1, width)[places_sent].astype(jnp.float32)]
    all_gather x4 -> x0, waiting for transfers between devices: 199 us -> none  [the longest x1 110 us: local(): lax.all_gather(query_weight, 'expert', axis=0, tiled=True)]
    dot_general x26 -> x43, matrix products: 277 us -> 393 us  [the longest x4 71.4 us: take(): return jnp.einsum('sjt,std->sjd', pick, source, preferred_element_type=f32)]
    psum x2, blocking collectives: 6.61 us -> 105 us  [the longest x1 63.4 us: local_block(): model_gains = lax.psum(gains[:2 * width], 'expert')]
    unnamed x2 -> x0, blocking collectives: 96.2 us -> none
    all_gather x2 -> x0, blocking collectives: 71.7 us -> none  [the longest x1 40.9 us: local(): lax.all_gather(attn_gain, 'expert', axis=0, tiled=True)]
  transfers between devices with their start and end apart: 15 -> 8, of which waited for: 10 -> 2; matrix products, arithmetic and copies ran while one was open for 14% -> 10% of each run, Pallas kernels for 0% -> 6%
where the time goes in v1:
time: 2200 us; the launch traced here: 2190 us
  Pallas kernels  788 us (36%)
  waiting for transfers between devices  712 us (32%)
  matrix products  401 us (18%)
  blocking collectives  105 us (5%)
  other arithmetic  103 us (5%)
  local copies, waits for them, and re-layouts  57.7 us (3%)
    reduce_scatter x4, waiting for transfers between devices, local_block(): lax.psum_scatter(v, 'expert', scatter_dimension=0, tiled=True)  712 us
    pallas_call x3, Pallas kernels, all_gather_blocks(): pl.pallas_call(functools.partial(gather_kernel, n, share), out_shape=[jax...  454 us
    pallas_call x2, Pallas kernels, reduce_scatter_rows(): pl.pallas_call(scatter_kernel, out_shape=jax.ShapeDtypeStruct((2 * rows,...  334 us
    dot_general x4, matrix products, take(): return jnp.einsum('sjt,std->sjd', pick, source, preferred_element_type=f32)  71.4 us
    psum x1, blocking collectives, local_block(): model_gains = lax.psum(gains[:2 * width], 'expert')  63.4 us
    dot_general x2, matrix products, put(): jnp.einsum('sjt,sjd->std', pick_both, both, preferred_element_type=f32)  51.8 us
  transfers between devices with their start and end apart: 8, of which 2 were waited for; matrix products, arithmetic and copies ran while one was open for 10% of the time, Pallas kernels for 6%

profile of v1, /device:TPU:10, one launch (start us, length us, event | category | flops | bytes accessed | tf_op | source)
XLA Modules:
  0.0 2193.7 jit_solution(3943753996196917188)
XLA Ops:
  11.8 169.5 %gather_blocks.3 = (bf16[2048,2048]{1,0:T(8,128)(2,1)}, bf16[2048,256]{1,0:T(8,128)(2,1)}, bf16[2048,256]{1,0:T(8,128)(2,1)}, bf16[2048,2048]{1,0:T(8,128)(2,1)}, f32[1536,128]{1,0:T(8,128)}) custom-call(bf16[128,2048]{1,0:T(8,128)(2,1)} %refs_0_.2, bf16[128,256]{1,0:T(8,128)(2,1)} %refs_1_.1, bf16[128,256]{1,0:T(8,128)(2,1)} %refs_2_.1, ...), custom_call_target="tpu_custom_call" | custom-call | tf_op jit(solution)/shard_map/gather_blocks/pallas_call | solution.py:496
  269.0 141.5 %gather_blocks.5 = bf16[8192,2048]{1,0:T(8,128)(2,1)} custom-call(bf16[512,2048]{1,0:T(8,128)(2,1)} %refs_0_.3), custom_call_target="tpu_custom_call" | custom-call | tf_op jit(solution)/shard_map/gather_blocks/pallas_call | solution.py:496
  410.5 18.2 multiply_convert_fusion
  428.7 17.7 multiply_convert_fusion.1
  453.0 143.0 %gather_blocks.4 = bf16[8192,2048]{1,0:T(8,128)(2,1)} custom-call(bf16[512,2048]{1,0:T(8,128)(2,1)} %multiply_convert_fusion.4.refs_0_), custom_call_target="tpu_custom_call" | custom-call | tf_op jit(solution)/shard_map/gather_blocks/pallas_call | solution.py:496
  596.0 17.9 convolution_convert_fusion
  613.9 17.6 convolution_convert_fusion.1
  631.5 10.8 fusion.47
  666.0 14.8 multiply_reduce_fusion.6
  689.2 10.8 multiply_reduce_fusion.5
  708.2 25.5 %fusion.11 = bf16[16,512,2048]{2,1,0:T(8,128)(2,1)} fusion(bf16[16,160,2048]{2,1,0:T(8,128)(2,1)} %bitcast.336, bf16[16,160,2048]{2,1,0:T(8,128)(2,1)} %bitcast.335, pred[16,160,512]{2,1,0:T(32,128)(4,1)S(1)} %copy-done.42, pred[16,160,512]{2,1,0:T(32,128)(4,1)S(1)} %copy-done.41), kind=kOutput, calls=%fused_computation.15 | convolution fusion | flops 10798759936 | bytes 57147392 | tf_op jit(solution)/shard_map/sjt,sjd->std/dot_general | solution.py:765
  733.7 166.8 %scatter_rows.2 = f32[512,2048]{1,0:T(8,128)} custom-call(bf16[8192,2048]{1,0:T(8,128)(2,1)} %bitcast.269), custom_call_target="tpu_custom_call" | custom-call | tf_op jit(solution)/shard_map/scatter_rows/pallas_call | solution.py:638
  900.5 12.0 fusion.59
  922.6 12.4 add_convert_fusion.1
  935.0 12.3 add_convert_fusion
  947.3 26.3 %fusion.8 = bf16[16,512,2048]{2,1,0:T(8,128)(2,1)} fusion(bf16[16,160,2048]{2,1,0:T(8,128)(2,1)} %bitcast.271, bf16[16,160,2048]{2,1,0:T(8,128)(2,1)} %bitcast.270, pred[16,160,512]{2,1,0:T(32,128)(4,1)} %iota_compare_fusion, pred[16,160,512]{2,1,0:T(32,128)(4,1)} %iota_compare_fusion.3), kind=kOutput, calls=%fused_computation.14 | convolution fusion | flops 10798759936 | bytes 57147392 | tf_op jit(solution)/shard_map/sjt,sjd->std/dot_general | solution.py:765
  973.6 167.4 %scatter_rows.3 = f32[512,2048]{1,0:T(8,128)} custom-call(bf16[8192,2048]{1,0:T(8,128)(2,1)} %bitcast.268), custom_call_target="tpu_custom_call" | custom-call | tf_op jit(solution)/shard_map/scatter_rows/pallas_call | solution.py:638
  1173.6 10.6 fusion.18
  1206.8 15.5 copy.132
  1280.9 13.3 fusion.82
  1304.5 41.7 %psum.38 = f32[256]{0:T(256)S(1)} all-reduce(f32[256]{0:T(256)S(1)} %pad_maximum_fusion.10), channel_id=1, replica_groups=mesh['expert'=16,'tensor'=2] {'expert','tensor'}, use_global_device_ids=true, to_apply=%region_34.35 | all-reduce | flops 256 | bytes 2048 | tf_op jit(solution)/shard_map/psum | solution.py:815
  1404.0 63.4 %psum.37 = f32[4096]{0:T(1024)S(1)} all-reduce(f32[4096]{0:T(1024)S(1)} %pad_maximum_fusion.9), channel_id=1, replica_groups=mesh['expert'=16,'tensor'=2] {'expert'}, use_global_device_ids=true, to_apply=%region_29.30 | all-reduce | flops 4096 | bytes 32768 | tf_op jit(solution)/shard_map/psum | solution.py:816
  1474.8 356.9 %reduce-scatter.11.cloned.1.call-done = f32[128,2048]{1,0:T(8,128)} async-done(((f32[2048,2048]{1,0:T(8,128)}), f32[128,2048]{1,0:T(8,128)}) %reduce-scatter.11.cloned.1.call-update) | async-done | bytes 1048592 | tf_op jit(solution)/shard_map/reduce_scatter | solution.py:812
  1831.7 354.9 %reduce-scatter.5.cloned.1.call-done = f32[128,2048]{1,0:T(8,128)} async-done(((f32[2048,2048]{1,0:T(8,128)}), f32[128,2048]{1,0:T(8,128)}) %reduce-scatter.5.cloned.1.call-update) | async-done | bytes 1048592 | tf_op jit(solution)/shard_map/reduce_scatter | solution.py:812
  (368 shorter events, 336.9 us)
Async XLA Ops:
  7.2 181.1 %copy-start.5 = (bf16[512,2048]{1,0:T(8,128)(2,1)S(1)}, bf16[512,2048]{1,0:T(8,128)(2,1)}, u32[]{:S(2)}) copy-start(bf16[512,2048]{1,0:T(8,128)(2,1)} %param.16) | copy-start | bytes 6291460
  7.2 439.2 %all-reduce.6.cloned.1.call-start = ((), (), s32[]{:S(2)}) async-start(), calls=%async_computation.5 | async-start | bytes 8388608 | tf_op jit(solution)/shard_map/psum | solution.py:725
  182.2 267.1 %copy-start.55 = (f32[16,1,128]{2,1,0:T(1,128)}, f32[16,1,128]{2,1,0:T(1,128)S(1)}, u32[]{:S(2)}) copy-start(f32[16,1,128]{2,1,0:T(1,128)S(1)} %get-tuple-element.64) | copy-start | bytes 24580
  188.1 59.8 %copy-start.73 = (f32[128]{0:T(128)}, f32[128]{0:T(128)S(1)}, u32[]{:S(2)}) copy-start(f32[128]{0:T(128)S(1)} %mul.506) | copy-start | bytes 1540
  188.2 60.3 %copy-start.71 = (f32[128]{0:T(128)}, f32[128]{0:T(128)S(1)}, u32[]{:S(2)}) copy-start(f32[128]{0:T(128)S(1)} %mul.521) | copy-start | bytes 1540
  262.8 351.1 %copy-start.29 = (s32[16,512]{1,0:T(8,128)}, s32[16,512]{1,0:T(8,128)S(1)}, u32[]{:S(2)}) copy-start(s32[16,512]{1,0:T(8,128)S(1)} %fusion.81) | copy-start | bytes 98308
  265.3 163.5 %copy-start.47 = (f32[16,160]{1,0:T(8,128)}, f32[16,160]{1,0:T(8,128)S(1)}, u32[]{:S(2)}) copy-start(f32[16,160]{1,0:T(8,128)S(1)} %select_reduce_fusion.3) | copy-start | bytes 30724
  265.6 330.4 %copy-start.31 = (s32[16,512]{1,0:T(8,128)}, s32[16,512]{1,0:T(8,128)S(1)}, u32[]{:S(2)}) copy-start(s32[16,512]{1,0:T(8,128)S(1)} %fusion.79) | copy-start | bytes 98308
  268.3 142.2 %copy-start.49 = (f32[16,160]{1,0:T(8,128)}, f32[16,160]{1,0:T(8,128)S(1)}, u32[]{:S(2)}) copy-start(f32[16,160]{1,0:T(8,128)S(1)} %select_reduce_fusion.2) | copy-start | bytes 30724
  449.2 146.8 %copy-start.64 = (f32[512]{0:T(512)}, f32[512]{0:T(512)S(1)}, u32[]{:S(2)}) copy-start(f32[512]{0:T(512)S(1)} %add_rsqrt_fusion.2) | copy-start | bytes 6148
  631.5 20.1 slice-start.7
  631.5 20.1 slice-start.8
  659.5 29.6 %slice-start.4 = ((s8[10485760]{0:T(1024)(128)(4,1)}), s8[2097152]{0:T(1024)(128)(4,1)S(1)}, s32[]{:S(2)}) async-start(s8[10485760]{0:T(1024)(128)(4,1)} %bitcast.284), calls=%async_computation.16 | async-start | bytes 4194304
  666.0 23.1 %slice-start.5 = ((s8[10485760]{0:T(1024)(128)(4,1)}), s8[4194304]{0:T(1024)(128)(4,1)S(1)}, s32[]{:S(2)}) async-start(s8[10485760]{0:T(1024)(128)(4,1)} %bitcast.284), calls=%async_computation.17 | async-start | bytes 8388608
  666.0 23.1 %slice-start.6 = ((s8[10485760]{0:T(1024)(128)(4,1)}), s8[4194304]{0:T(1024)(128)(4,1)S(1)}, s32[]{:S(2)}) async-start(s8[10485760]{0:T(1024)(128)(4,1)} %bitcast.284), calls=%async_computation.18 | async-start | bytes 8388608
  1196.4 72.9 %all-to-all-start = ((f32[16,2,512]{2,1,0:T(2,128)}), f32[16,2,512]{2,1,0:T(2,128)S(1)}, u32[]{:S(2)}, u32[]{:S(2)}) async-start(f32[16,2,512]{2,1,0:T(2,128)} %copy.133), calls=%async_computation.4 | async-start | bytes 131072 | tf_op jit(solution)/shard_map/all_to_all | solution.py:770
  1206.7 192.7 %all-reduce.10.cloned.1.call-start = ((), (), s32[]{:S(2)}) async-start(), calls=%async_computation.11 | async-start | bytes 131072 | tf_op jit(solution)/shard_map/psum | solution.py:771
  1270.0 130.9 %all-reduce.8.cloned.1.call-start = ((), (), s32[]{:S(2)}) async-start(), calls=%async_computation.6 | async-start | bytes 4194304 | tf_op jit(solution)/shard_map/psum | solution.py:804
  1275.9 198.9 %reduce-scatter.7.cloned.1.call-start = ((), (), s32[]{:S(2)}) async-start(), calls=%async_computation.8 | async-start | bytes 2228224 | tf_op jit(solution)/shard_map/reduce_scatter | solution.py:812
  1278.4 196.4 %reduce-scatter.9.cloned.1.call-start = ((), (), s32[]{:S(2)}) async-start(), calls=%async_computation.9 | async-start | bytes 2228224 | tf_op jit(solution)/shard_map/reduce_scatter | solution.py:812
  1280.8 550.8 %reduce-scatter.11.cloned.1.call-start = ((), (), s32[]{:S(2)}) async-start(), calls=%async_computation.10 | async-start | bytes 17825792 | tf_op jit(solution)/shard_map/reduce_scatter | solution.py:812
  1294.3 892.3 %reduce-scatter.5.cloned.1.call-start = ((), (), s32[]{:S(2)}) async-start(), calls=%async_computation.7 | async-start | bytes 17825792 | tf_op jit(solution)/shard_map/reduce_scatter | solution.py:812
  1347.3 18.9 slice-start.13
  1347.3 18.9 slice-start.14
  (85 other events, 569.3 us)
Sparse Core Ops, SparseCore 0:
  246.9 28.3 all-reduce.5
  1270.1 18.8 all-reduce.9
  1291.4 22.4 all-reduce.7
  1316.6 73.2 reduce-scatter.6
  1392.6 78.1 reduce-scatter.8
  1473.5 358.0 reduce-scatter.10
  1834.5 352.0 reduce-scatter.4

commit v2 on v1

--- a/solution.py
+++ b/solution.py
@@ -5,6 +5,53 @@
 from jax.experimental import pallas as pl
 from jax.experimental.pallas import tpu as pltpu
 from jax.sharding import PartitionSpec as P
+
+NAME_D = 'd'
+NAME_EXPERT = 'expert'
+NAME_FIN = 'fin'
+NAME_GATHER_BLOCKS = 'gather_blocks'
+NAME_NGQK_KND_QNGD = 'ngqk,knd->qngd'
+NAME_NGQK_QNGD_KND = 'ngqk,qngd->knd'
+NAME_P = 'p'
+NAME_Q = 'q'
+NAME_QNGD_KND_NGQK = 'qngd,knd->ngqk'
+NAME_RD_FD_RF = 'rd,fd->rf'
+NAME_RD_RF_DF = 'rd,rf->df'
+NAME_RF_DF_RD = 'rf,df->rd'
+NAME_RF_RD_FD = 'rf,rd->fd'
+NAME_S0 = 's0'
+NAME_S1 = 's1'
+NAME_S2 = 's2'
+NAME_S3 = 's3'
+NAME_SCATTER_GRADS = 'scatter_grads'
+NAME_SCATTER_ROWS = 'scatter_rows'
+NAME_SIB = 'sib'
+NAME_SJT_SJD_STD = 'sjt,sjd->std'
+NAME_SJT_STD_SJD = 'sjt,std->sjd'
+NAME_SLED_LDF_SLEF = 'sled,ldf->slef'
+NAME_SLED_LFD_SLEF = 'sled,lfd->slef'
+NAME_SLED_SLEF_LDF = 'sled,slef->ldf'
+NAME_SLEF_LDF_SLED = 'slef,ldf->sled'
+NAME_SLEF_LFD_SLED = 'slef,lfd->sled'
+NAME_SLEF_SLED_LFD = 'slef,sled->lfd'
+NAME_TD_DH_TH = 'td,dh->th'
+NAME_TD_TH_DH = 'td,th->dh'
+NAME_TENSOR = 'tensor'
+NAME_TH_DH_TD = 'th,dh->td'
+NAME_U = 'u'
+NAME_W = 'w'
+NAME_X2 = 'x2'
+NAME_XP = 'xP'
+NAME_XQ = 'xQ'
+NAME_XQR = 'xQr'
+NAME_XD = 'xd'
+NAME_XX = 'xx'
+NAME_Y2 = 'y2'
+NAME_YP = 'yP'
+NAME_YPR = 'yPr'
+NAME_YQ = 'yQ'
+NAME_YD = 'yd'
+NAME_YY = 'yy'
 
 HEAD_SIZE = 128
 
@@ -54,20 +101,20 @@
 
 def scores_of(grouped_heads, keys_low, allowed):
     scaled = jnp.einsum(
-        "qngd,knd->ngqk", grouped_heads, keys_low, preferred_element_type=jnp.float32
+        NAME_QNGD_KND_NGQK, grouped_heads, keys_low, preferred_element_type=jnp.float32
     ) * HEAD_SIZE ** (-0.5)
     return jnp.where(allowed, scaled, NEG)
 
 
 def to_owners(fetcher, experts, capacity):
     picked = fetcher(jnp.arange(experts * capacity, dtype=jnp.int32)).reshape(experts, capacity, -1)
-    arrived = lax.all_to_all(picked, "expert", split_axis=0, concat_axis=0, tiled=True)
+    arrived = lax.all_to_all(picked, NAME_EXPERT, split_axis=0, concat_axis=0, tiled=True)
     return arrived
 
 
 def to_sources(expert_rows, places_sent):
     width = expert_rows.shape[-1]
-    returned = lax.all_to_all(expert_rows, "expert", split_axis=0, concat_axis=0, tiled=True)
+    returned = lax.all_to_all(expert_rows, NAME_EXPERT, split_axis=0, concat_axis=0, tiled=True)
     return returned.reshape(-1, width)[places_sent].astype(jnp.float32)
 
 
@@ -90,14 +137,14 @@
     cotangent,
 ):
     gathered = (
-        lax.all_gather(query_weight, "expert", axis=0, tiled=True),
-        lax.all_gather(key_weight, "expert", axis=0, tiled=True),
-        lax.all_gather(value_matrix, "expert", axis=0, tiled=True),
-        lax.all_gather(output_weight, "expert", axis=0, tiled=True),
-        lax.all_gather(attn_gain, "expert", axis=0, tiled=True),
-        lax.all_gather(moe_gain, "expert", axis=0, tiled=True),
-        lax.all_gather(query_gain, "expert", axis=0, tiled=True),
-        lax.all_gather(key_gain, "expert", axis=0, tiled=True),
+        lax.all_gather(query_weight, NAME_EXPERT, axis=0, tiled=True),
+        lax.all_gather(key_weight, NAME_EXPERT, axis=0, tiled=True),
+        lax.all_gather(value_matrix, NAME_EXPERT, axis=0, tiled=True),
+        lax.all_gather(output_weight, NAME_EXPERT, axis=0, tiled=True),
+        lax.all_gather(attn_gain, NAME_EXPERT, axis=0, tiled=True),
+        lax.all_gather(moe_gain, NAME_EXPERT, axis=0, tiled=True),
+        lax.all_gather(query_gain, NAME_EXPERT, axis=0, tiled=True),
+        lax.all_gather(key_gain, NAME_EXPERT, axis=0, tiled=True),
     )
     full_query, full_key, full_value, full_output = (
         gathered[0],
@@ -140,15 +187,15 @@
     probs_low = (weights / totals).astype(jnp.bfloat16)
     log_total = row_peak + jnp.log(totals)
     mixed_low = (
-        jnp.einsum("ngqk,knd->qngd", probs_low, values_low, preferred_element_type=jnp.float32)
+        jnp.einsum(NAME_NGQK_KND_QNGD, probs_low, values_low, preferred_element_type=jnp.float32)
         .reshape(tok_rows, heads_here * HEAD_SIZE)
         .astype(jnp.bfloat16)
     )
-    attn_part = jnp.einsum("th,dh->td", mixed_low, full_output, preferred_element_type=jnp.float32)
-    hidden = inputs + lax.psum(attn_part, "tensor")
+    attn_part = jnp.einsum(NAME_TH_DH_TD, mixed_low, full_output, preferred_element_type=jnp.float32)
+    hidden = inputs + lax.psum(attn_part, NAME_TENSOR)
     unit_moe, factor_moe = rms_parts(hidden)
     normed_moe = (unit_moe * gain_moe).astype(jnp.bfloat16)
-    n_devices = lax.axis_size("expert")
+    n_devices = lax.axis_size(NAME_EXPERT)
     local_experts = gate_proj.shape[0]
     experts = n_devices * local_experts
     top_count = routes.shape[1]
@@ -174,18 +221,18 @@
         n_devices, local_experts, capacity, -1
     )
     gate_value = jnp.einsum(
-        "sled,ldf->slef", arrived, gate_proj, preferred_element_type=jnp.float32
-    )
-    up_value = jnp.einsum("sled,ldf->slef", arrived, up_proj, preferred_element_type=jnp.float32)
+        NAME_SLED_LDF_SLEF, arrived, gate_proj, preferred_element_type=jnp.float32
+    )
+    up_value = jnp.einsum(NAME_SLED_LDF_SLEF, arrived, up_proj, preferred_element_type=jnp.float32)
     hidden_act = (jax.nn.silu(gate_value) * up_value).astype(jnp.bfloat16)
     out_rows = jnp.einsum(
-        "slef,lfd->sled", hidden_act, down_proj, preferred_element_type=jnp.float32
+        NAME_SLEF_LFD_SLED, hidden_act, down_proj, preferred_element_type=jnp.float32
     ).astype(jnp.bfloat16)
     per_choice = to_sources(out_rows.reshape(experts, capacity, -1), places_sent).reshape(
         tok_rows, top_count, -1
     )
     moe_part = jnp.sum(gate_weights[:, :, None] * per_choice, axis=1)
-    moe_out = lax.psum(moe_part.astype(jnp.bfloat16), "tensor").astype(jnp.float32)
+    moe_out = lax.psum(moe_part.astype(jnp.bfloat16), NAME_TENSOR).astype(jnp.float32)
     block_out = (hidden + moe_out).astype(jnp.bfloat16)
     upstream = cotangent.astype(jnp.float32)
     gate_part = jnp.sum(per_choice * upstream[:, None, :], axis=-1)
@@ -204,10 +251,10 @@
         n_devices, local_experts, capacity, -1
     )
     grad_act = jnp.einsum(
-        "sled,lfd->slef", grad_rows, down_proj, preferred_element_type=jnp.float32
+        NAME_SLED_LFD_SLEF, grad_rows, down_proj, preferred_element_type=jnp.float32
     )
     grad_down = jnp.einsum(
-        "slef,sled->lfd", hidden_act, grad_rows, preferred_element_type=jnp.float32
+        NAME_SLEF_SLED_LFD, hidden_act, grad_rows, preferred_element_type=jnp.float32
     )
     sigmoid_gate = jax.nn.sigmoid(gate_value)
     grad_up_low = (grad_act * gate_value * sigmoid_gate).astype(jnp.bfloat16)
@@ -215,43 +262,43 @@
         grad_act * up_value * sigmoid_gate * (1.0 + gate_value * (1.0 - sigmoid_gate))
     ).astype(jnp.bfloat16)
     grad_gate_w = jnp.einsum(
-        "sled,slef->ldf", arrived, grad_gate_low, preferred_element_type=jnp.float32
+        NAME_SLED_SLEF_LDF, arrived, grad_gate_low, preferred_element_type=jnp.float32
     )
     grad_up_w = jnp.einsum(
-        "sled,slef->ldf", arrived, grad_up_low, preferred_element_type=jnp.float32
+        NAME_SLED_SLEF_LDF, arrived, grad_up_low, preferred_element_type=jnp.float32
     )
     grad_in = jnp.einsum(
-        "slef,ldf->sled", grad_gate_low, gate_proj, preferred_element_type=jnp.float32
+        NAME_SLEF_LDF_SLED, grad_gate_low, gate_proj, preferred_element_type=jnp.float32
     )
     grad_in = (
         grad_in
-        + jnp.einsum("slef,ldf->sled", grad_up_low, up_proj, preferred_element_type=jnp.float32)
+        + jnp.einsum(NAME_SLEF_LDF_SLED, grad_up_low, up_proj, preferred_element_type=jnp.float32)
     ).astype(jnp.bfloat16)
     grad_choice = to_sources(grad_in.reshape(experts, capacity, -1), places_sent).reshape(
         tok_rows, top_count, -1
     )
     grad_moe_part = jnp.sum(grad_choice, axis=1)
-    grad_normed_moe, grad_gates = lax.psum((grad_moe_part, gate_part), "tensor")
+    grad_normed_moe, grad_gates = lax.psum((grad_moe_part, gate_part), NAME_TENSOR)
     grad_moe_gain = jnp.sum(grad_normed_moe * unit_moe, axis=0)
     grad_hidden = upstream + norm_back(grad_normed_moe * gain_moe, unit_moe, factor_moe)
     grad_attn_low = grad_hidden.astype(jnp.bfloat16)
     back_query, back_key, back_value, back_output = (full_query, full_key, full_value, full_output)
     grad_mixed = jnp.einsum(
-        "td,dh->th", grad_attn_low, back_output, preferred_element_type=jnp.float32
+        NAME_TD_DH_TH, grad_attn_low, back_output, preferred_element_type=jnp.float32
     )
     grad_mixed_low = grad_mixed.astype(jnp.bfloat16).reshape(
         tok_rows, kv_here, query_group_width, HEAD_SIZE
     )
     grad_output_w = jnp.einsum(
-        "td,th->dh", grad_attn_low, mixed_low, preferred_element_type=jnp.float32
+        NAME_TD_TH_DH, grad_attn_low, mixed_low, preferred_element_type=jnp.float32
     )
     scores = scores_of(grouped_heads, keys_low, allowed)
     prob_full = jnp.exp(scores - log_total)
     grad_probs = jnp.einsum(
-        "qngd,knd->ngqk", grad_mixed_low, values_low, preferred_element_type=jnp.float32
+        NAME_QNGD_KND_NGQK, grad_mixed_low, values_low, preferred_element_type=jnp.float32
     )
     grad_values = jnp.einsum(
-        "ngqk,qngd->knd",
+        NAME_NGQK_QNGD_KND,
         prob_full.astype(jnp.bfloat16),
         grad_mixed_low,
         preferred_element_type=jnp.float32,
@@ -261,12 +308,12 @@
     score_scale = HEAD_SIZE ** (-0.5)
     grad_queries = (
         jnp.einsum(
-            "ngqk,knd->qngd", grad_scores, keys_low, preferred_element_type=jnp.float32
+            NAME_NGQK_KND_QNGD, grad_scores, keys_low, preferred_element_type=jnp.float32
         ).reshape(tok_rows, heads_here, HEAD_SIZE)
         * score_scale
     )
     grad_keys = (
-        jnp.einsum("ngqk,qngd->knd", grad_scores, grouped_heads, preferred_element_type=jnp.float32)
+        jnp.einsum(NAME_NGQK_QNGD_KND, grad_scores, grouped_heads, preferred_element_type=jnp.float32)
         * score_scale
     )
     grad_qhead = rotate(grad_queries, cos_table, -sin_table)
@@ -285,39 +332,39 @@
     )
     grad_value_low = grad_values.reshape(tok_rows, kv_here * HEAD_SIZE)
     grad_normed_part = jnp.einsum(
-        "th,dh->td", grad_query_low, back_query, preferred_element_type=jnp.float32
+        NAME_TH_DH_TD, grad_query_low, back_query, preferred_element_type=jnp.float32
     )
     grad_normed_part = grad_normed_part + jnp.einsum(
-        "th,dh->td", grad_key_low, back_key, preferred_element_type=jnp.float32
+        NAME_TH_DH_TD, grad_key_low, back_key, preferred_element_type=jnp.float32
     )
     grad_normed_part = grad_normed_part + jnp.einsum(
-        "th,dh->td", grad_value_low, back_value, preferred_element_type=jnp.float32
+        NAME_TH_DH_TD, grad_value_low, back_value, preferred_element_type=jnp.float32
     )
     grad_query_w = jnp.einsum(
-        "td,th->dh", normalized_input, grad_query_low, preferred_element_type=jnp.float32
+        NAME_TD_TH_DH, normalized_input, grad_query_low, preferred_element_type=jnp.float32
     )
     grad_key_w = jnp.einsum(
-        "td,th->dh", normalized_input, grad_key_low, preferred_element_type=jnp.float32
+        NAME_TD_TH_DH, normalized_input, grad_key_low, preferred_element_type=jnp.float32
     )
     grad_value_w = jnp.einsum(
-        "td,th->dh", normalized_input, grad_value_low, preferred_element_type=jnp.float32
+        NAME_TD_TH_DH, normalized_input, grad_value_low, preferred_element_type=jnp.float32
     )
     grad_normed, query_gain_sum, key_gain_sum = (
-        lax.psum(grad_normed_part.astype(jnp.bfloat16), "tensor").astype(jnp.float32),
-        lax.psum(query_gain_part.astype(jnp.bfloat16), "tensor").astype(jnp.float32),
-        lax.psum(key_gain_part.astype(jnp.bfloat16), "tensor").astype(jnp.float32),
+        lax.psum(grad_normed_part.astype(jnp.bfloat16), NAME_TENSOR).astype(jnp.float32),
+        lax.psum(query_gain_part.astype(jnp.bfloat16), NAME_TENSOR).astype(jnp.float32),
+        lax.psum(key_gain_part.astype(jnp.bfloat16), NAME_TENSOR).astype(jnp.float32),
     )
     grad_attn_gain_part = jnp.sum(grad_normed * unit_attn, axis=0)
     grad_tokens = grad_hidden + norm_back(grad_normed * gain_attn, unit_attn, factor_attn)
     shares = (
-        lax.psum_scatter(grad_query_w, "expert", scatter_dimension=0, tiled=True),
-        lax.psum_scatter(grad_key_w, "expert", scatter_dimension=0, tiled=True),
-        lax.psum_scatter(grad_value_w, "expert", scatter_dimension=0, tiled=True),
-        lax.psum_scatter(grad_output_w, "expert", scatter_dimension=0, tiled=True),
-        lax.psum_scatter(grad_attn_gain_part, "expert", scatter_dimension=0, tiled=True),
-        lax.psum_scatter(grad_moe_gain, "expert", scatter_dimension=0, tiled=True),
-        lax.psum_scatter(query_gain_sum, "expert", scatter_dimension=0, tiled=True),
-        lax.psum_scatter(key_gain_sum, "expert", scatter_dimension=0, tiled=True),
+        lax.psum_scatter(grad_query_w, NAME_EXPERT, scatter_dimension=0, tiled=True),
+        lax.psum_scatter(grad_key_w, NAME_EXPERT, scatter_dimension=0, tiled=True),
+        lax.psum_scatter(grad_value_w, NAME_EXPERT, scatter_dimension=0, tiled=True),
+        lax.psum_scatter(grad_output_w, NAME_EXPERT, scatter_dimension=0, tiled=True),
+        lax.psum_scatter(grad_attn_gain_part, NAME_EXPERT, scatter_dimension=0, tiled=True),
+        lax.psum_scatter(grad_moe_gain, NAME_EXPERT, scatter_dimension=0, tiled=True),
+        lax.psum_scatter(query_gain_sum, NAME_EXPERT, scatter_dimension=0, tiled=True),
+        lax.psum_scatter(key_gain_sum, NAME_EXPERT, scatter_dimension=0, tiled=True),
     )
     return (
         block_out,
@@ -341,7 +388,7 @@
 ZS, YS, XS = 4, 2, 2
 
 def place():
-    e = lax.axis_index("expert"); c = lax.axis_index("tensor")
+    e = lax.axis_index(NAME_EXPERT); c = lax.axis_index(NAME_TENSOR)
     return e // 4, (e // 2) % 2, e % 2, c
 
 def ident(z, y, x, c):
@@ -374,15 +421,15 @@
         if share:
             base = base + c * rows[a]
         half = rows[a] // 2
-        if part == "w":
+        if part == NAME_W:
             return pl.ds(pl.multiple_of(base, 16), rows[a])
-        return pl.ds(pl.multiple_of(base + (0 if part == "p" else half), 16), half)
+        return pl.ds(pl.multiple_of(base + (0 if part == NAME_P else half), 16), half)
     def src_own(a, part):
         half = rows[a] // 2
         base = c * rows[a] if share else 0
-        if part == "w":
+        if part == NAME_W:
             return ins[a].at[pl.ds(base, rows[a]), :]
-        off = 0 if part == "p" else half
+        off = 0 if part == NAME_P else half
         return ins[a].at[pl.ds(base + off, half), :]
     keys = {}
     def num(k):
@@ -417,8 +464,8 @@
             each(lambda a: cp(k, a, b, part, dev).wait_recv())
         if cond is None: go()
         else: pl.when(cond)(go)
-    send(z < 3, ("u", 0), me, "w", zu, True)
-    send(z > 0, ("d", 0), me, "w", zd, True)
+    send(z < 3, (NAME_U, 0), me, NAME_W, zu, True)
+    send(z > 0, (NAME_D, 0), me, NAME_W, zd, True)
     slots = [(0, 0)] + [(d, sg) for d in (1, 2, 3) for sg in (-1, 1)]
     def cond_of(d, sg):
         if d == 0: return None
@@ -426,27 +473,27 @@
     def A(d, sg):
         s = z + sg * d; cnd = cond_of(d, sg); own = d == 0
         b = bid(s, y, x)
-        send(cnd, ("xP", d, sg), b, "p", xn, own)
-        send(cnd, ("yQ", d, sg), b, "q", yn, own)
-        send(cnd, ("xQ", d, sg), b, "q", xn, own)
-        send(cnd, ("yP", d, sg), b, "p", yn, own)
+        send(cnd, (NAME_XP, d, sg), b, NAME_P, xn, own)
+        send(cnd, (NAME_YQ, d, sg), b, NAME_Q, yn, own)
+        send(cnd, (NAME_XQ, d, sg), b, NAME_Q, xn, own)
+        send(cnd, (NAME_YP, d, sg), b, NAME_P, yn, own)
         if share and not own:
-            send(cnd, ("s0", d, sg), b, "w", sib)
+            send(cnd, (NAME_S0, d, sg), b, NAME_W, sib)
     def B(d, sg):
         s = z + sg * d; cnd = cond_of(d, sg)
-        recv(cnd, ("xP", d, sg), bid(s, y, 1 - x), "p", xn)
-        send(cnd, ("yPr", d, sg), bid(s, y, 1 - x), "p", yn)
-        recv(cnd, ("yQ", d, sg), bid(s, 1 - y, x), "q", yn)
-        send(cnd, ("xQr", d, sg), bid(s, 1 - y, x), "q", xn)
+        recv(cnd, (NAME_XP, d, sg), bid(s, y, 1 - x), NAME_P, xn)
+        send(cnd, (NAME_YPR, d, sg), bid(s, y, 1 - x), NAME_P, yn)
+        recv(cnd, (NAME_YQ, d, sg), bid(s, 1 - y, x), NAME_Q, yn)
+        send(cnd, (NAME_XQR, d, sg), bid(s, 1 - y, x), NAME_Q, xn)
     def C(d, sg):
         s = z + sg * d; cnd = cond_of(d, sg)
-        recv(cnd, ("xQ", d, sg), bid(s, y, 1 - x), "q", xn)
-        if share: send(cnd, ("s1", d, sg), bid(s, y, 1 - x), "w", sib)
-        recv(cnd, ("yP", d, sg), bid(s, 1 - y, x), "p", yn)
-        if share: send(cnd, ("s2", d, sg), bid(s, 1 - y, x), "w", sib)
-        recv(cnd, ("yPr", d, sg), bid(s, 1 - y, 1 - x), "p", yn)
-        recv(cnd, ("xQr", d, sg), bid(s, 1 - y, 1 - x), "q", xn)
-        if share: send(cnd, ("s3", d, sg), bid(s, 1 - y, 1 - x), "w", sib)
+        recv(cnd, (NAME_XQ, d, sg), bid(s, y, 1 - x), NAME_Q, xn)
+        if share: send(cnd, (NAME_S1, d, sg), bid(s, y, 1 - x), NAME_W, sib)
+        recv(cnd, (NAME_YP, d, sg), bid(s, 1 - y, x), NAME_P, yn)
+        if share: send(cnd, (NAME_S2, d, sg), bid(s, 1 - y, x), NAME_W, sib)
+        recv(cnd, (NAME_YPR, d, sg), bid(s, 1 - y, 1 - x), NAME_P, yn)
+        recv(cnd, (NAME_XQR, d, sg), bid(s, 1 - y, 1 - x), NAME_Q, xn)
+        if share: send(cnd, (NAME_S3, d, sg), bid(s, 1 - y, 1 - x), NAME_W, sib)
     A(0, 0)
     each(lambda a: own_in(a).start())
     each(lambda a: own_in(a).wait())
@@ -454,13 +501,13 @@
     B(0, 0)
     prev = [(0, 0)]
     for d in (1, 2, 3):
-        recv(z - d >= 0, ("u", d - 1), bid(z - d, y, x), "w", zd)
+        recv(z - d >= 0, (NAME_U, d - 1), bid(z - d, y, x), NAME_W, zd)
         if d < 3:
-            send((z - d >= 0) & (z < 3), ("u", d), bid(z - d, y, x), "w", zu)
+            send((z - d >= 0) & (z < 3), (NAME_U, d), bid(z - d, y, x), NAME_W, zu)
         A(d, -1)
-        recv(z + d <= 3, ("d", d - 1), bid(z + d, y, x), "w", zu)
+        recv(z + d <= 3, (NAME_D, d - 1), bid(z + d, y, x), NAME_W, zu)
         if d < 3:
-            send((z + d <= 3) & (z > 0), ("d", d), bid(z + d, y, x), "w", zd)
+            send((z + d <= 3) & (z > 0), (NAME_D, d), bid(z + d, y, x), NAME_W, zd)
         A(d, 1)
         B(d, -1); B(d, 1)
         for p in prev: C(*p)
@@ -478,10 +525,10 @@
                         pltpu.make_async_remote_copy(src_ref=r, dst_ref=r, send_sem=ss.at[i, a], recv_sem=rs.at[i, a], device_id=sib, device_id_type=MESH).wait_recv()
                 if cnd is None: go()
                 else: pl.when(cnd)(go)
-            if d: sibwait(("s0", d, sg), bid(s, y, x))
-            sibwait(("s1", d, sg), bid(s, y, 1 - x))
-            sibwait(("s2", d, sg), bid(s, 1 - y, x))
-            sibwait(("s3", d, sg), bid(s, 1 - y, 1 - x))
+            if d: sibwait((NAME_S0, d, sg), bid(s, y, x))
+            sibwait((NAME_S1, d, sg), bid(s, y, 1 - x))
+            sibwait((NAME_S2, d, sg), bid(s, 1 - y, x))
+            sibwait((NAME_S3, d, sg), bid(s, 1 - y, 1 - x))
     for cond, k, b, part, dev, own in sends:
         def go():
             each(lambda a: cp(k, a, b, part, dev, own).wait_send())
@@ -500,7 +547,7 @@
         scratch_shapes=[pltpu.VMEM(a.shape, a.dtype) for a in arrays] + [
             pltpu.SemaphoreType.DMA((NKEYS, n)), pltpu.SemaphoreType.DMA((NKEYS, n)), pltpu.SemaphoreType.DMA((n, 2))],
         compiler_params=pltpu.CompilerParams(collective_id=cid, has_side_effects=True),
-        name="gather_blocks",
+        name=NAME_GATHER_BLOCKS,
     )(*arrays)
 
 
@@ -541,7 +588,7 @@
         cnd = cond_of(d, sg); s = z + sg * d
         for q, b in enumerate(blocks(s)):
             guard(cnd, lambda: load(b).start())
-            send(cnd, ("sib", d, sg, q), part_at(b, 1 - c), SR.at[b], sib)
+            send(cnd, (NAME_SIB, d, sg, q), part_at(b, 1 - c), SR.at[b], sib)
     def sum_into(dst, row0, terms, n=half):
         def step(i, _):
             r = pl.ds(row0 + i * CH, CH)
@@ -557,36 +604,36 @@
         def go():
             for q, b in enumerate((m, xx, yy, dd)):
                 load(b).wait()
-                rc(("sib", d, sg, q), SR.at[b], SR.at[b], sib).wait_recv()
+                rc((NAME_SIB, d, sg, q), SR.at[b], SR.at[b], sib).wait_recv()
             sum_into(A.at[dd], 0, [(SR.at[dd], 0)], rows)
         guard(cnd, go)
-        send(cnd, ("yd", i), A.at[dd, Ph, :], RP.at[s, 1], yn)
-        send(cnd, ("xd", i), A.at[dd, Qh, :], RQ.at[s, 1], xn)
+        send(cnd, (NAME_YD, i), A.at[dd, Ph, :], RP.at[s, 1], yn)
+        send(cnd, (NAME_XD, i), A.at[dd, Qh, :], RQ.at[s, 1], xn)
         guard(cnd, lambda: (sum_into(A.at[yy], 0, [(SR.at[yy], 0)]), sum_into(A.at[xx], half, [(SR.at[xx], half)]))and None)
-        send(cnd, ("yy", i), A.at[yy, Ph, :], RP.at[s, 0], yn)
-        send(cnd, ("xx", i), A.at[xx, Qh, :], RQ.at[s, 0], xn)
+        send(cnd, (NAME_YY, i), A.at[yy, Ph, :], RP.at[s, 0], yn)
+        send(cnd, (NAME_XX, i), A.at[xx, Qh, :], RQ.at[s, 0], xn)
     def S2(i):
         d, sg = SLOTS[i]; cnd = cond_of(d, sg); s = z + sg * d
         m, xx, yy, dd = blocks(s)
-        recv(cnd, ("yd", i), RP.at[s, 1], yn)
+        recv(cnd, (NAME_YD, i), RP.at[s, 1], yn)
         guard(cnd, lambda: sum_into(A.at[xx], 0, [(SR.at[xx], 0), (RP.at[s, 1], 0)]))
-        send(cnd, ("x2", i), A.at[xx, Ph, :], RP2.at[s], xn)
-        recv(cnd, ("xd", i), RQ.at[s, 1], xn)
+        send(cnd, (NAME_X2, i), A.at[xx, Ph, :], RP2.at[s], xn)
+        recv(cnd, (NAME_XD, i), RQ.at[s, 1], xn)
         guard(cnd, lambda: sum_into(A.at[yy], half, [(SR.at[yy], half), (RQ.at[s, 1], 0)]))
-        send(cnd, ("y2", i), A.at[yy, Qh, :], RQ2.at[s], yn)
+        send(cnd, (NAME_Y2, i), A.at[yy, Qh, :], RQ2.at[s], yn)
     def S3(i):
         d, sg = SLOTS[i]; cnd = cond_of(d, sg); s = z + sg * d
         m = blocks(s)[0]
-        recv(cnd, ("yy", i), RP.at[s, 0], yn)
-        recv(cnd, ("xx", i), RQ.at[s, 0], xn)
-        recv(cnd, ("x2", i), RP2.at[s], xn)
-        recv(cnd, ("y2", i), RQ2.at[s], yn)
+        recv(cnd, (NAME_YY, i), RP.at[s, 0], yn)
+        recv(cnd, (NAME_XX, i), RQ.at[s, 0], xn)
+        recv(cnd, (NAME_X2, i), RP2.at[s], xn)
+        recv(cnd, (NAME_Y2, i), RQ2.at[s], yn)
         base_p = [(SR.at[m], 0), (RP.at[s, 0], 0), (RP2.at[s], 0)]
         base_q = [(SR.at[m], half), (RQ.at[s, 0], 0), (RQ2.at[s], 0)]
         if d:
             back = (z > 0) if sg > 0 else (z < 3)
             Z = ZU if sg > 0 else ZD
-            name = "u" if sg > 0 else "d"
+            name = NAME_U if sg > 0 else NAME_D
             dn, up = (zd, zu) if sg > 0 else (zu, zd)
             has = d <= 2
             def plain():
@@ -599,8 +646,8 @@
                 pl.when(cnd)(plain)
             send(cnd, (name, d - 1), A.at[m], Z.at[d - 1], up)
         else:
-            recv(z > 0, ("u", 0), ZU.at[0], zd)
-            recv(z < 3, ("d", 0), ZD.at[0], zu)
+            recv(z > 0, (NAME_U, 0), ZU.at[0], zd)
+            recv(z < 3, (NAME_D, 0), ZD.at[0], zu)
             lo = jnp.where(z > 0, 1.0, 0.0); hi = jnp.where(z < 3, 1.0, 0.0)
             def emit(row0, terms, flags):
                 def step(i, _):
@@ -618,8 +665,8 @@
                     emit(0, base_p, fl); emit(half, base_q, fl)
             mine = out.at[pl.ds(pl.multiple_of(c * rows, 16), rows), :]
             other = out.at[pl.ds(pl.multiple_of((1 - c) * rows, 16), rows), :]
-            send(None, ("fin",), mine, mine, sib)
-            recv(None, ("fin",), other, sib)
+            send(None, (NAME_FIN,), mine, mine, sib)
+            recv(None, (NAME_FIN,), other, sib)
     n = len(SLOTS)
     for i in range(n + 2):
         if i < n: S1(i)
@@ -646,8 +693,175 @@
             pltpu.VMEM((3, rows, width), bf), pltpu.VMEM((3, rows, width), bf),
             pltpu.SemaphoreType.DMA((16,)), pltpu.SemaphoreType.DMA((NK,)), pltpu.SemaphoreType.DMA((NK,))],
         compiler_params=pltpu.CompilerParams(collective_id=cid, has_side_effects=True, vmem_limit_bytes=67043328),
-        name="scatter_rows",
+        name=NAME_SCATTER_ROWS,
     )(part)
+
+
+STEP = 16
+
+def grads_kernel(n, *refs):
+    ins, small = refs[:n], refs[n]
+    outs, seen = refs[n + 1:2 * n + 1], refs[2 * n + 1]
+    A, RP, RP2, RQ, RQ2, ZU, ZD, V, ls, ss, rs, fs, fr = refs[2 * n + 2:]
+    z, y, x, c = place()
+    rows = A.shape[1]; half = rows // 2
+    devices = small.shape[0]
+    me = (z * 4 + y * 2 + x) * 2 + c
+    widths = [r.shape[1] for r in ins]
+    offs = [sum(widths[:a]) for a in range(n)]
+    def peer(i):
+        p = lax.rem(me + i, devices)
+        return p, (p // 2, p % 2)
+    bar = pltpu.get_barrier_semaphore()
+    def hello(i, _):
+        pl.semaphore_signal(bar, inc=1, device_id=peer(i)[1], device_id_type=MESH)
+        return 0
+    def cond_of(d, sg):
+        if d == 0: return None
+        return (z - d >= 0) if sg < 0 else (z + d <= 3)
+    def guard(cnd, go):
+        if cnd is None: go()
+        else: pl.when(cnd)(go)
+    def blocks(s):
+        b = s * 4
+        return b + y * 2 + x, b + y * 2 + 1 - x, b + (1 - y) * 2 + x, b + (1 - y) * 2 + 1 - x
+    def loads(b):
+        return [pltpu.make_async_copy(ins[a].at[pl.ds(pl.multiple_of(b * rows, 16), rows), :],
+                                      A.at[b, :, pl.ds(offs[a], widths[a])], ls.at[b, a]) for a in range(n)]
+    for d, sg in SLOTS:
+        for b in blocks(z + sg * d):
+            guard(cond_of(d, sg), lambda: [l.start() for l in loads(b)] and None)
+    lax.fori_loop(1, devices, hello, 0)
+    pl.semaphore_wait(bar, devices - 1)
+    def piece(i, to):
+        p, dev = peer(i)
+        return pltpu.make_async_remote_copy(src_ref=small.at[p], dst_ref=seen.at[me], send_sem=fs.at[i], recv_sem=fr.at[i],
+                                            device_id=dev, device_id_type=MESH)
+    def piece_in(i):
+        q = lax.rem(me - i + devices, devices)
+        return pltpu.make_async_remote_copy(src_ref=small.at[q], dst_ref=seen.at[q], send_sem=fs.at[i], recv_sem=fr.at[i],
+                                            device_id=(q // 2, q % 2), device_id_type=MESH)
+    def piece_go(i, _):
+        piece(i, 0).start(); return 0
+    lax.fori_loop(1, devices, piece_go, 0)
+    seen[me] = small[me]
+    xn, yn, zu, zd = ident(z, y, 1 - x, c), ident(z, 1 - y, x, c), ident(z + 1, y, x, c), ident(z - 1, y, x, c)
+    keys = {}
+    def num(k): return keys.setdefault(k, len(keys))
+    sent = []
+    def rc(k, src, dst, dev):
+        i = num(k)
+        return pltpu.make_async_remote_copy(src_ref=src, dst_ref=dst, send_sem=ss.at[i], recv_sem=rs.at[i], device_id=dev, device_id_type=MESH)
+    def send(cnd, k, src, dst, dev):
+        guard(cnd, lambda: rc(k, src, dst, dev).start())
+        sent.append((cnd, k, src, dst, dev))
+    def recv(cnd, k, dst, dev):
+        guard(cnd, lambda: rc(k, dst, dst, dev).wait_recv())
+    Ph, Qh = pl.ds(0, half), pl.ds(half, half)
+    def add_into(store, terms, n_rows=half):
+        def step(i, _):
+            acc = None
+            for t, off in terms:
+                v = t[pl.ds(off + i * STEP, STEP), :].astype(jnp.float32)
+                acc = v if acc is None else acc + v
+            store(i * STEP, acc)
+            return 0
+        lax.fori_loop(0, n_rows // STEP, step, 0)
+    def to(dst, row0):
+        def store(r, acc):
+            dst[pl.ds(row0 + r, STEP), :] = acc.astype(dst.dtype)
+        return store
+    def to_outs(row0):
+        def store(r, acc):
+            for a in range(n):
+                outs[a][pl.ds(row0 + r, STEP), :] = acc[:, offs[a]:offs[a] + widths[a]]
+        return store
+    def S1(i):
+        d, sg = SLOTS[i]; cnd = cond_of(d, sg); s = z + sg * d
+        m, xx, yy, dd = blocks(s)
+        guard(cnd, lambda: [l.wait() for b in (m, xx, yy, dd) for l in loads(b)] and None)
+        send(cnd, (NAME_YD, i), A.at[dd, Ph, :], RP.at[s, 1], yn)
+        send(cnd, (NAME_XD, i), A.at[dd, Qh, :], RQ.at[s, 1], xn)
+        send(cnd, (NAME_YY, i), A.at[yy, Ph, :], RP.at[s, 0], yn)
+        send(cnd, (NAME_XX, i), A.at[xx, Qh, :], RQ.at[s, 0], xn)
+    def S2(i):
+        d, sg = SLOTS[i]; cnd = cond_of(d, sg); s = z + sg * d
+        m, xx, yy, dd = blocks(s)
+        recv(cnd, (NAME_YD, i), RP.at[s, 1], yn)
+        guard(cnd, lambda: add_into(to(A.at[xx], 0), [(A.at[xx], 0), (RP.at[s, 1], 0)]))
+        send(cnd, (NAME_X2, i), A.at[xx, Ph, :], RP2.at[s], xn)
+        recv(cnd, (NAME_XD, i), RQ.at[s, 1], xn)
+        guard(cnd, lambda: add_into(to(A.at[yy], half), [(A.at[yy], half), (RQ.at[s, 1], 0)]))
+        send(cnd, (NAME_Y2, i), A.at[yy, Qh, :], RQ2.at[s], yn)
+    def S3(i):
+        d, sg = SLOTS[i]; cnd = cond_of(d, sg); s = z + sg * d
+        m = blocks(s)[0]
+        recv(cnd, (NAME_YY, i), RP.at[s, 0], yn)
+        recv(cnd, (NAME_XX, i), RQ.at[s, 0], xn)
+        recv(cnd, (NAME_X2, i), RP2.at[s], xn)
+        recv(cnd, (NAME_Y2, i), RQ2.at[s], yn)
+        base_p = [(A.at[m], 0), (RP.at[s, 0], 0), (RP2.at[s], 0)]
+        base_q = [(A.at[m], half), (RQ.at[s, 0], 0), (RQ2.at[s], 0)]
+        if d:
+            slot = s - 1 if sg > 0 else s
+            back = (z > 0) if sg > 0 else (z < 3)
+            Z, name, dn, up = (ZU, NAME_U, zd, zu) if sg > 0 else (ZD, NAME_D, zu, zd)
+            def plain():
+                add_into(to(V.at[slot], 0), base_p); add_into(to(V.at[slot], half), base_q)
+            if d <= 2:
+                recv(cnd & back, (name, d), Z.at[d], dn)
+                def carried():
+                    add_into(to(V.at[slot], 0), base_p + [(Z.at[d], 0)]); add_into(to(V.at[slot], half), base_q + [(Z.at[d], half)])
+                pl.when(cnd & back)(carried)
+                pl.when(cnd & jnp.logical_not(back))(plain)
+            else:
+                pl.when(cnd)(plain)
+            send(cnd, (name, d - 1), V.at[slot], Z.at[d - 1], up)
+        else:
+            recv(z > 0, (NAME_U, 0), ZU.at[0], zd)
+            recv(z < 3, (NAME_D, 0), ZD.at[0], zu)
+            for cc, zs in ((z == 0, (ZD,)), (z == 3, (ZU,)), ((z > 0) & (z < 3), (ZU, ZD))):
+                def emit(zs=zs):
+                    add_into(to_outs(0), base_p + [(q.at[0], 0) for q in zs])
+                    add_into(to_outs(half), base_q + [(q.at[0], half) for q in zs])
+                pl.when(cc)(emit)
+    k = len(SLOTS)
+    for i in range(k + 2):
+        if i < k: S1(i)
+        if 0 <= i - 1 < k: S2(i - 1)
+        if 0 <= i - 2 < k: S3(i - 2)
+    for cnd, key, src, dst, dev in sent:
+        guard(cnd, lambda: rc(key, src, dst, dev).wait_send())
+    def piece_end(i, _):
+        piece(i, 0).wait_send()
+        piece_in(i).wait_recv()
+        return 0
+    lax.fori_loop(1, devices, piece_end, 0)
+    assert len(keys) <= NG, len(keys)
+
+NG = 56
+def reduce_scatter_grads(parts, small, cid):
+    n = len(parts)
+    rows = parts[0].shape[0] // (small.shape[0] // 2)
+    half = rows // 2
+    width = sum(p.shape[1] for p in parts)
+    bf, f32 = parts[0].dtype, jnp.float32
+    vmem, hbm = pl.BlockSpec(memory_space=pltpu.VMEM), pl.BlockSpec(memory_space=pltpu.HBM)
+    res = pl.pallas_call(
+        functools.partial(grads_kernel, n),
+        out_shape=[jax.ShapeDtypeStruct((rows, p.shape[1]), f32) for p in parts] + [jax.ShapeDtypeStruct(small.shape, f32)],
+        in_specs=[hbm] * n + [vmem], out_specs=[vmem] * (n + 1),
+        scratch_shapes=[
+            pltpu.VMEM((16, rows, width), bf),
+            pltpu.VMEM((4, 2, half, width), bf), pltpu.VMEM((4, half, width), bf),
+            pltpu.VMEM((4, 2, half, width), bf), pltpu.VMEM((4, half, width), bf),
+            pltpu.VMEM((3, rows, width), f32), pltpu.VMEM((3, rows, width), f32), pltpu.VMEM((3, rows, width), f32),
+            pltpu.SemaphoreType.DMA((16, n)), pltpu.SemaphoreType.DMA((NG,)), pltpu.SemaphoreType.DMA((NG,)),
+            pltpu.SemaphoreType.DMA((small.shape[0],)), pltpu.SemaphoreType.DMA((small.shape[0],))],
+        compiler_params=pltpu.CompilerParams(collective_id=cid, has_side_effects=True, vmem_limit_bytes=67043328),
+        name=NAME_SCATTER_GRADS,
+    )(*parts, small)
+    return res[:n], res[n]
 
 def tables(routes_all, weights_all, first, local_experts, capacity):
     n, rows, top = routes_all.shape
@@ -719,17 +933,17 @@
     probs_low = (weights / totals).astype(bf16)
     log_total = row_peak + jnp.log(totals)
     mixed_low = (
-        jnp.einsum("ngqk,knd->qngd", probs_low, values_low, preferred_element_type=f32)
+        jnp.einsum(NAME_NGQK_KND_QNGD, probs_low, values_low, preferred_element_type=f32)
         .reshape(tok_rows, heads_here * HEAD_SIZE).astype(bf16))
-    attn_part = jnp.einsum("th,dh->td", mixed_low, full_output, preferred_element_type=f32)
-    hidden = inputs + lax.psum(attn_part, "tensor")
+    attn_part = jnp.einsum(NAME_TH_DH_TD, mixed_low, full_output, preferred_element_type=f32)
+    hidden = inputs + lax.psum(attn_part, NAME_TENSOR)
     unit_moe, factor_moe = rms_parts(hidden)
     normed_moe = (unit_moe * gain_moe).astype(bf16)
 
     local_experts = gate_proj.shape[0]
     experts = n_chips * local_experts
     capacity = assigned * 5 // (4 * experts)
-    chip = lax.axis_index("expert")
+    chip = lax.axis_index(NAME_EXPERT)
     picks, scale = tables(routes_all, weights_all, chip * local_experts, local_experts, capacity)
     (x_all,) = all_gather_blocks([normed_moe], 3, share=True)
     x_all = x_all.reshape(n_chips, tok_rows, width)
@@ -738,7 +952,7 @@
     for l in range(local_experts):
         pick = picks[l].astype(bf16)
         def take(source):
-            return jnp.einsum("sjt,std->sjd", pick, source, preferred_element_type=f32)
+            return jnp.einsum(NAME_SJT_STD_SJD, pick, source, preferred_element_type=f32)
         w_slot = scale[l].reshape(-1, 1)
         xs = take(x_all).astype(bf16).reshape(-1, width)
         dys = (scale[l] * take(dy_all)).astype(bf16).reshape(-1, width)
@@ -747,50 +961,45 @@
         sigmoid_gate = jax.nn.sigmoid(gate_value)
         act = (gate_value * sigmoid_gate * up_value).astype(bf16)
         y_rows.append((w_slot * jnp.dot(act, down_proj[l], preferred_element_type=f32)).astype(bf16))
-        grad_act = jnp.einsum("rd,fd->rf", dys, down_proj[l], preferred_element_type=f32)
+        grad_act = jnp.einsum(NAME_RD_FD_RF, dys, down_proj[l], preferred_element_type=f32)
         gates_slot = jnp.sum(act.astype(f32) * grad_act, axis=-1, keepdims=True) / jnp.where(w_slot > 0, w_slot, 1.0)
         gates_tok.append(jnp.sum(jnp.where(picks[l], gates_slot.reshape(n_chips, capacity, 1), 0.0), axis=1))
         up_low = (grad_act * gate_value * sigmoid_gate).astype(bf16)
         gate_low = (grad_act * up_value * sigmoid_gate * (1.0 + gate_value * (1.0 - sigmoid_gate))).astype(bf16)
-        dx = jnp.einsum("rf,df->rd", gate_low, gate_proj[l], preferred_element_type=f32)
-        dx = dx + jnp.einsum("rf,df->rd", up_low, up_proj[l], preferred_element_type=f32)
+        dx = jnp.einsum(NAME_RF_DF_RD, gate_low, gate_proj[l], preferred_element_type=f32)
+        dx = dx + jnp.einsum(NAME_RF_DF_RD, up_low, up_proj[l], preferred_element_type=f32)
         dx_rows.append(dx.astype(bf16))
         grads.append((
-            jnp.einsum("rd,rf->df", xs, gate_low, preferred_element_type=f32),
-            jnp.einsum("rd,rf->df", xs, up_low, preferred_element_type=f32),
-            jnp.einsum("rf,rd->fd", act, dys, preferred_element_type=f32)))
+            jnp.einsum(NAME_RD_RF_DF, xs, gate_low, preferred_element_type=f32),
+            jnp.einsum(NAME_RD_RF_DF, xs, up_low, preferred_element_type=f32),
+            jnp.einsum(NAME_RF_RD_FD, act, dys, preferred_element_type=f32)))
     pick_both = jnp.concatenate(picks, axis=1).astype(bf16)
     def put(rows):
         both = jnp.concatenate([r.reshape(n_chips, capacity, width) for r in rows], axis=1)
-        return jnp.einsum("sjt,sjd->std", pick_both, both, preferred_element_type=f32).astype(bf16).reshape(-1, width)
+        return jnp.einsum(NAME_SJT_SJD_STD, pick_both, both, preferred_element_type=f32).astype(bf16).reshape(-1, width)
     grad_normed_moe = reduce_scatter_rows(put(dx_rows), 4)
     moe_out = reduce_scatter_rows(put(y_rows), 5)
     grad_gate_w, grad_up_w, grad_down = (jnp.stack([g[i] for g in grads]) for i in range(3))
     block_out = (hidden + moe_out).astype(bf16)
-    gates_back = lax.all_to_all(jnp.stack(gates_tok, axis=1), "expert", split_axis=0, concat_axis=0, tiled=True)
-    gates_back = lax.psum(gates_back, "tensor").reshape(experts, tok_rows)
-    grad_gates = jnp.sum(
-        jnp.where(routes[:, :, None] == jnp.arange(experts, dtype=jnp.int32), gates_back.T[:, None, :], 0.0), axis=-1)
-
     upstream = cotangent.astype(f32)
     grad_moe_gain = jnp.sum(grad_normed_moe * unit_moe, axis=0)
     grad_hidden = upstream + norm_back(grad_normed_moe * gain_moe, unit_moe, factor_moe)
     grad_attn_low = grad_hidden.astype(bf16)
-    grad_mixed = jnp.einsum("td,dh->th", grad_attn_low, full_output, preferred_element_type=f32)
+    grad_mixed = jnp.einsum(NAME_TD_DH_TH, grad_attn_low, full_output, preferred_element_type=f32)
     grad_mixed_low = grad_mixed.astype(bf16).reshape(tok_rows, kv_here, query_group_width, HEAD_SIZE)
-    grad_output_w = jnp.einsum("td,th->dh", grad_attn_low, mixed_low, preferred_element_type=f32)
+    grad_output_w = jnp.einsum(NAME_TD_TH_DH, grad_attn_low, mixed_low, preferred_element_type=f32)
     scores = scores_of(grouped_heads, keys_low, allowed)
     prob_full = jnp.exp(scores - log_total)
-    grad_probs = jnp.einsum("qngd,knd->ngqk", grad_mixed_low, values_low, preferred_element_type=f32)
+    grad_probs = jnp.einsum(NAME_QNGD_KND_NGQK, grad_mixed_low, values_low, preferred_element_type=f32)
     grad_values = jnp.einsum(
-        "ngqk,qngd->knd", prob_full.astype(bf16), grad_mixed_low, preferred_element_type=f32).astype(bf16)
+        NAME_NGQK_QNGD_KND, prob_full.astype(bf16), grad_mixed_low, preferred_element_type=f32).astype(bf16)
     row_delta = jnp.sum(prob_full * grad_probs, axis=-1, keepdims=True)
     grad_scores = (prob_full * (grad_probs - row_delta)).astype(bf16)
     score_scale = HEAD_SIZE ** (-0.5)
     grad_queries = (
-        jnp.einsum("ngqk,knd->qngd", grad_scores, keys_low, preferred_element_type=f32)
+        jnp.einsum(NAME_NGQK_KND_QNGD, grad_scores, keys_low, preferred_element_type=f32)
         .reshape(tok_rows, heads_here, HEAD_SIZE) * score_scale)
-    grad_keys = jnp.einsum("ngqk,qngd->knd", grad_scores, grouped_heads, preferred_element_type=f32) * score_scale
+    grad_keys = jnp.einsum(NAME_NGQK_QNGD_KND, grad_scores, grouped_heads, preferred_element_type=f32) * score_scale
     grad_qhead = rotate(grad_queries, cos_table, -sin_table)
     grad_khead = rotate(grad_keys, cos_table, -sin_table)
     query_gain_part = jnp.sum(grad_qhead * query_unit, axis=(0, 1))
@@ -798,70 +1007,79 @@
     grad_query_low = norm_back(grad_qhead * gain_query, query_unit, query_factor).astype(bf16).reshape(tok_rows, -1)
     grad_key_low = norm_back(grad_khead * gain_key, key_unit, key_factor).astype(bf16).reshape(tok_rows, -1)
     grad_value_low = grad_values.reshape(tok_rows, -1)
-    grad_normed_part = jnp.einsum("th,dh->td", grad_query_low, full_query, preferred_element_type=f32)
-    grad_normed_part = grad_normed_part + jnp.einsum("th,dh->td", grad_key_low, full_key, preferred_element_type=f32)
-    grad_normed_part = grad_normed_part + jnp.einsum("th,dh->td", grad_value_low, full_value, preferred_element_type=f32)
-    grad_normed = lax.psum(grad_normed_part.astype(bf16), "tensor").astype(f32)
+    grad_normed_part = jnp.einsum(NAME_TH_DH_TD, grad_query_low, full_query, preferred_element_type=f32)
+    grad_normed_part = grad_normed_part + jnp.einsum(NAME_TH_DH_TD, grad_key_low, full_key, preferred_element_type=f32)
+    grad_normed_part = grad_normed_part + jnp.einsum(NAME_TH_DH_TD, grad_value_low, full_value, preferred_element_type=f32)
+    grad_normed = lax.psum(grad_normed_part.astype(bf16), NAME_TENSOR).astype(f32)
     grad_attn_gain_part = jnp.sum(grad_normed * unit_attn, axis=0)
     grad_tokens = grad_hidden + norm_back(grad_normed * gain_attn, unit_attn, factor_attn)
 
-    grad_query_w = jnp.einsum("td,th->dh", normalized_input, grad_query_low, preferred_element_type=f32)
-    grad_key_w = jnp.einsum("td,th->dh", normalized_input, grad_key_low, preferred_element_type=f32)
-    grad_value_w = jnp.einsum("td,th->dh", normalized_input, grad_value_low, preferred_element_type=f32)
-    shares = tuple(
-        lax.psum_scatter(v, "expert", scatter_dimension=0, tiled=True)
-        for v in (grad_query_w, grad_key_w, grad_value_w, grad_output_w))
-    gains = jnp.concatenate([grad_attn_gain_part, grad_moe_gain, query_gain_part, key_gain_part])
-    head_gains = lax.psum(gains[2 * width:], ("expert", "tensor"))
-    model_gains = lax.psum(gains[:2 * width], "expert")
-    def own(v):
-        size = v.shape[0] // n_chips
-        return lax.dynamic_slice_in_dim(v, chip * size, size, 0)
+    def weight_grad(left, right):
+        return jnp.dot(left.T, right, preferred_element_type=f32).astype(bf16)
+    gates_rows = local_experts * tok_rows // lanes
+    head_row = jnp.concatenate([query_gain_part.reshape(n_chips, per), key_gain_part.reshape(n_chips, per)], axis=1)
+    pieces = jnp.concatenate(
+        [
+            jnp.stack(gates_tok, axis=1).reshape(n_chips, gates_rows, lanes),
+            grad_attn_gain_part.reshape(n_chips, gain_rows, lanes), grad_moe_gain.reshape(n_chips, gain_rows, lanes),
+            jnp.pad(head_row, ((0, 0), (0, lanes - 2 * per)))[:, None, :],
+        ], axis=1)
+    pieces = jnp.repeat(jnp.pad(pieces, ((0, 0), (0, -pieces.shape[1] % 8), (0, 0))), 2, axis=0)
+    shares, seen = reduce_scatter_grads(
+        [weight_grad(normalized_input, grad_query_low), weight_grad(normalized_input, grad_key_low),
+         weight_grad(normalized_input, grad_value_low), weight_grad(grad_attn_low, mixed_low)], pieces, 6)
+    gates_back = jnp.sum(seen[:, :gates_rows].reshape(n_chips, 2, local_experts, tok_rows), axis=1).reshape(experts, tok_rows)
+    grad_gates = jnp.sum(
+        jnp.where(routes[:, :, None] == jnp.arange(experts, dtype=jnp.int32), gates_back.T[:, None, :], 0.0), axis=-1)
+    gains = jnp.sum(seen[:, gates_rows:], axis=0)
+    own_attn = 0.5 * gains[:gain_rows].reshape(-1)
+    own_moe = 0.5 * gains[gain_rows:2 * gain_rows].reshape(-1)
+    head_gains = gains[2 * gain_rows]
     return (
         block_out, grad_tokens, *shares,
-        own(model_gains[:width]), own(model_gains[width:]), own(head_gains[:HEAD_SIZE]), own(head_gains[HEAD_SIZE:]),
+        own_attn, own_moe, head_gains[:per], head_gains[per:2 * per],
         grad_gate_w, grad_up_w, grad_down, grad_gates,
     )
 
 
 def solution(mesh):
-    wide = mesh.shape["expert"] == ZS * YS * XS and mesh.shape["tensor"] == 2
+    wide = mesh.shape[NAME_EXPERT] == ZS * YS * XS and mesh.shape[NAME_TENSOR] == 2
     return jax.shard_map(
         local_block if wide else local,
         mesh=mesh,
         in_specs=(
-            P("expert", None),
-            P("expert"),
-            P("expert"),
-            P("expert"),
-            P("expert"),
-            P("expert", "tensor"),
-            P("expert", "tensor"),
-            P("expert", "tensor"),
-            P("expert", "tensor"),
-            P("expert", None, "tensor"),
-            P("expert", None, "tensor"),
-            P("expert", "tensor", None),
-            P("expert", None),
-            P("expert", None),
-            P("expert"),
-            P("expert", None),
+            P(NAME_EXPERT, None),
+            P(NAME_EXPERT),
+            P(NAME_EXPERT),
+            P(NAME_EXPERT),
+            P(NAME_EXPERT),
+            P(NAME_EXPERT, NAME_TENSOR),
+            P(NAME_EXPERT, NAME_TENSOR),
+            P(NAME_EXPERT, NAME_TENSOR),
+            P(NAME_EXPERT, NAME_TENSOR),
+            P(NAME_EXPERT, None, NAME_TENSOR),
+            P(NAME_EXPERT, None, NAME_TENSOR),
+            P(NAME_EXPERT, NAME_TENSOR, None),
+            P(NAME_EXPERT, None),
+            P(NAME_EXPERT, None),
+            P(NAME_EXPERT),
+            P(NAME_EXPERT, None),
         ),
         out_specs=(
-            P("expert", None),
-            P("expert", None),
-            P("expert", "tensor"),
-            P("expert", "tensor"),
-            P("expert", "tensor"),
-            P("expert", "tensor"),
-            P("expert"),
-            P("expert"),
-            P("expert"),
-            P("expert"),
-            P("expert", None, "tensor"),
-            P("expert", None, "tensor"),
-            P("expert", "tensor", None),
-            P("expert", None),
+            P(NAME_EXPERT, None),
+            P(NAME_EXPERT, None),
+            P(NAME_EXPERT, NAME_TENSOR),
+            P(NAME_EXPERT, NAME_TENSOR),
+            P(NAME_EXPERT, NAME_TENSOR),
+            P(NAME_EXPERT, NAME_TENSOR),
+            P(NAME_EXPERT),
+            P(NAME_EXPERT),
+            P(NAME_EXPERT),
+            P(NAME_EXPERT),
+            P(NAME_EXPERT, None, NAME_TENSOR),
+            P(NAME_EXPERT, None, NAME_TENSOR),
+            P(NAME_EXPERT, NAME_TENSOR, None),
+            P(NAME_EXPERT, None),
         ),
         check_vma=False,
     )

time: 2200 us -> 1640 us (0.75); the launches traced: 2190 us -> 1610 us
  waiting for transfers between devices: 712 us -> 0.88 us
  Pallas kernels: 788 us -> 997 us
  blocking collectives: 105 us -> 0 us
  other arithmetic: 103 us -> 126 us
    reduce_scatter x4 -> x0, waiting for transfers between devices: 712 us -> none  [local_block(): lax.psum_scatter(v, 'expert', scatter_dimension=0, tiled=True)]
    pallas_call x0 -> x1, Pallas kernels: none -> 209 us  [reduce_scatter_grads(): pl.pallas_call(functools.partial(grads_kernel, n), out_shape=[jax.ShapeDt...]
    psum x2 -> x0, blocking collectives: 105 us -> none  [the longest x1 63.4 us: local_block(): model_gains = lax.psum(gains[:2 * width], 'expert')]
  transfers between devices with their start and end apart: 8 -> 2, of which waited for: 2 -> 1; matrix products, arithmetic and copies ran while one was open for 10% -> 5% of each run, Pallas kernels for 6% -> 9%
where the time goes in v2:
time: 1640 us; the launch traced here: 1610 us
  Pallas kernels  997 us (61%)
  matrix products  407 us (25%)
  other arithmetic  126 us (8%)
  local copies, waits for them, and re-layouts  62.1 us (4%)
    pallas_call x3, Pallas kernels, all_gather_blocks(): pl.pallas_call(functools.partial(gather_kernel, n, share), out_shape=[jax...  454 us
    pallas_call x2, Pallas kernels, reduce_scatter_rows(): pl.pallas_call(scatter_kernel, out_shape=jax.ShapeDtypeStruct((2 * rows,...  334 us
    pallas_call x1, Pallas kernels, reduce_scatter_grads(): pl.pallas_call(functools.partial(grads_kernel, n), out_shape=[jax.ShapeDt...  209 us
    dot_general x4, matrix products, take(): jnp.einsum(NAME_SJT_STD_SJD, pick, source, preferred_element_type=f32)  70.9 us
    dot_general x2, matrix products, put(): jnp.einsum(NAME_SJT_SJD_STD, pick_both, both, preferred_element_type=f32)  50.7 us
  transfers between devices with their start and end apart: 2, of which 1 were waited for; matrix products, arithmetic and copies ran while one was open for 5% of the time, Pallas kernels for 9%

profile of v2, /device:TPU:10, one launch (start us, length us, event | category | flops | bytes accessed | tf_op | source)
XLA Modules:
  0.0 1609.0 jit_solution(6435592482672771545)
XLA Ops:
  11.8 169.5 %gather_blocks.3 = (bf16[2048,2048]{1,0:T(8,128)(2,1)}, bf16[2048,256]{1,0:T(8,128)(2,1)}, bf16[2048,256]{1,0:T(8,128)(2,1)}, bf16[2048,2048]{1,0:T(8,128)(2,1)}, f32[1536,128]{1,0:T(8,128)}) custom-call(bf16[128,2048]{1,0:T(8,128)(2,1)} %refs_0_.2, bf16[128,256]{1,0:T(8,128)(2,1)} %refs_1_.1, bf16[128,256]{1,0:T(8,128)(2,1)} %refs_2_.1, ...), custom_call_target="tpu_custom_call" | custom-call | tf_op jit(solution)/shard_map/gather_blocks/pallas_call | solution.py:543
  269.3 141.5 %gather_blocks.5 = bf16[8192,2048]{1,0:T(8,128)(2,1)} custom-call(bf16[512,2048]{1,0:T(8,128)(2,1)} %refs_0_.3), custom_call_target="tpu_custom_call" | custom-call | tf_op jit(solution)/shard_map/gather_blocks/pallas_call | solution.py:543
  410.8 17.8 %multiply_convert_fusion = bf16[16,160,2048]{2,1,0:T(8,128)(2,1)} fusion(f32[16,160]{1,0:T(8,128)S(1)} %select_reduce_fusion.2, bf16[16,512,2048]{2,1,0:T(8,128)(2,1)} %bitcast.274, s32[16,512]{1,0:T(8,128)S(1)} %fusion.79), kind=kOutput, calls=%fused_computation.9 | convolution fusion | flops 5380505600 | bytes 44083200 | tf_op jit(solution)/shard_map/sjt,std->sjd/dot_general | solution.py:955
  428.6 17.7 %multiply_convert_fusion.1 = bf16[16,160,2048]{2,1,0:T(8,128)(2,1)} fusion(f32[16,160]{1,0:T(8,128)S(1)} %select_reduce_fusion.3, bf16[16,512,2048]{2,1,0:T(8,128)(2,1)} %bitcast.275, s32[16,512]{1,0:T(8,128)S(1)} %fusion.81), kind=kOutput, calls=%fused_computation.11 | convolution fusion | flops 5380505600 | bytes 44083200 | tf_op jit(solution)/shard_map/sjt,std->sjd/dot_general | solution.py:955
  452.8 143.0 %gather_blocks.4 = bf16[8192,2048]{1,0:T(8,128)(2,1)} custom-call(bf16[512,2048]{1,0:T(8,128)(2,1)} %multiply_convert_fusion.4.refs_0_), custom_call_target="tpu_custom_call" | custom-call | tf_op jit(solution)/shard_map/gather_blocks/pallas_call | solution.py:543
  595.9 17.7 %convolution_convert_fusion.2 = bf16[16,160,2048]{2,1,0:T(8,128)(2,1)} fusion(bf16[16,512,2048]{2,1,0:T(8,128)(2,1)} %bitcast.272, s32[16,512]{1,0:T(8,128)S(1)} %fusion.79), kind=kOutput, calls=%fused_computation.41 | convolution fusion | flops 5375262720 | bytes 44072960 | tf_op jit(solution)/shard_map/sjt,std->sjd/dot_general | solution.py:955
  613.6 17.8 %convolution_convert_fusion.3 = bf16[16,160,2048]{2,1,0:T(8,128)(2,1)} fusion(bf16[16,512,2048]{2,1,0:T(8,128)(2,1)} %bitcast.273, s32[16,512]{1,0:T(8,128)S(1)} %fusion.81), kind=kOutput, calls=%fused_computation.42 | convolution fusion | flops 5375262720 | bytes 44072960 | tf_op jit(solution)/shard_map/sjt,std->sjd/dot_general | solution.py:955
  631.4 10.8 fusion.47
  648.6 11.2 fusion.57
  690.6 11.8 fusion.59
  702.4 11.1 multiply_reduce_fusion.5
  713.5 11.4 convolution_bitcast_fusion.4
  725.0 11.8 fusion.49
  748.8 10.6 convolution_bitcast_fusion.2
  783.6 25.4 %fusion.11 = bf16[16,512,2048]{2,1,0:T(8,128)(2,1)} fusion(bf16[16,160,2048]{2,1,0:T(8,128)(2,1)} %bitcast.348, bf16[16,160,2048]{2,1,0:T(8,128)(2,1)} %bitcast.347, pred[16,160,512]{2,1,0:T(32,128)(4,1)S(1)} %copy-done.45, pred[16,160,512]{2,1,0:T(32,128)(4,1)S(1)} %copy-done.43), kind=kOutput, calls=%fused_computation.15 | convolution fusion | flops 10798759936 | bytes 57147392 | tf_op jit(solution)/shard_map/sjt,sjd->std/dot_general | solution.py:979
  809.0 166.8 %scatter_rows.2 = f32[512,2048]{1,0:T(8,128)} custom-call(bf16[8192,2048]{1,0:T(8,128)(2,1)} %bitcast.281), custom_call_target="tpu_custom_call" | custom-call | tf_op jit(solution)/shard_map/scatter_rows/pallas_call | solution.py:685
  975.9 13.6 add_convert_fusion.1
  989.6 12.4 add_convert_fusion
  1002.0 25.3 %fusion.8 = bf16[16,512,2048]{2,1,0:T(8,128)(2,1)} fusion(bf16[16,160,2048]{2,1,0:T(8,128)(2,1)} %bitcast.283, bf16[16,160,2048]{2,1,0:T(8,128)(2,1)} %bitcast.282, pred[16,160,512]{2,1,0:T(32,128)(4,1)S(1)} %copy-done.46, pred[16,160,512]{2,1,0:T(32,128)(4,1)S(1)} %copy-done.44), kind=kOutput, calls=%fused_computation.14 | convolution fusion | flops 10798759936 | bytes 57147392 | tf_op jit(solution)/shard_map/sjt,sjd->std/dot_general | solution.py:979
  1027.3 167.3 %scatter_rows.3 = f32[512,2048]{1,0:T(8,128)} custom-call(bf16[8192,2048]{1,0:T(8,128)(2,1)} %bitcast.280), custom_call_target="tpu_custom_call" | custom-call | tf_op jit(solution)/shard_map/scatter_rows/pallas_call | solution.py:685
  1227.0 10.8 fusion.18
  1278.9 17.1 %multiply_reduce_fusion.1 = (f32[512,16]{1,0:T(8,128)S(1)}, f32[512,16,128]{2,1,0:T(8,128)S(1)}) fusion(f32[512,16,128]{2,1,0:T(8,128)S(1)} %bitcast.279, f32[128]{0:T(128)S(1)} %copy-done.78, f32[512,16]{1,0:T(8,128)S(1)} %copy-done.23, f32[512,16,64]{2,1,0:T(8,128)} %get-tuple-element.57, f32[512,16,64]{2,1,0:T(8,128)S(1)} %get-tuple-element.56), kind=kLoop, calls=%fused_computation.68 | loop fusion | flops 5234688 | bytes 12648960 | tf_op jit(solution)/shard_map/reduce_sum | solution.py:71
  1322.7 14.9 copy.133
  1379.0 208.6 %scatter_grads.1 = (f32[128,2048]{1,0:T(8,128)}, f32[128,256]{1,0:T(8,128)}, f32[128,256]{1,0:T(8,128)}, f32[128,2048]{1,0:T(8,128)}, f32[32,16,128]{2,1,0:T(8,128)}) custom-call(bf16[2048,2048]{1,0:T(8,128)(2,1)} %convolution_convert_fusion.1.refs_0_, bf16[2048,256]{1,0:T(8,128)(2,1)} %convolution_convert_fusion.6.refs_1_, ...), custom_call_target="tpu_custom_call" | custom-call | tf_op jit(solution)/shard_map/scatter_grads/pallas_call | solution.py:850
  (363 shorter events, 327.5 us)
Async XLA Ops:
  7.2 181.1 %copy-start.6 = (bf16[512,2048]{1,0:T(8,128)(2,1)S(1)}, bf16[512,2048]{1,0:T(8,128)(2,1)}, u32[]{:S(2)}) copy-start(bf16[512,2048]{1,0:T(8,128)(2,1)} %param.16) | copy-start | bytes 6291460
  7.2 439.1 %all-reduce.7.cloned.1.call-start = ((), (), s32[]{:S(2)}) async-start(), calls=%async_computation | async-start | bytes 8388608 | tf_op jit(solution)/shard_map/psum | solution.py:939
  182.2 266.9 %copy-start.62 = (f32[16,1,128]{2,1,0:T(1,128)}, f32[16,1,128]{2,1,0:T(1,128)S(1)}, u32[]{:S(2)}) copy-start(f32[16,1,128]{2,1,0:T(1,128)S(1)} %get-tuple-element.74) | copy-start | bytes 24580
  188.2 59.5 %copy-start.79 = (f32[128]{0:T(128)}, f32[128]{0:T(128)S(1)}, u32[]{:S(2)}) copy-start(f32[128]{0:T(128)S(1)} %mul.510) | copy-start | bytes 1540
  188.3 59.9 %copy-start.77 = (f32[128]{0:T(128)}, f32[128]{0:T(128)S(1)}, u32[]{:S(2)}) copy-start(f32[128]{0:T(128)S(1)} %mul.525) | copy-start | bytes 1540
  192.2 14.4 copy-start.66
  192.5 14.2 copy-start.17
  246.5 1128.2 %all-reduce.9.cloned.1.call-start = ((), (), s32[]{:S(2)}) async-start(), calls=%async_computation.1 | async-start | bytes 4194304 | tf_op jit(solution)/shard_map/psum | solution.py:1013
  262.5 351.1 %copy-start.32 = (s32[16,512]{1,0:T(8,128)}, s32[16,512]{1,0:T(8,128)S(1)}, u32[]{:S(2)}) copy-start(s32[16,512]{1,0:T(8,128)S(1)} %fusion.81) | copy-start | bytes 98308
  265.0 163.6 %copy-start.52 = (f32[16,160]{1,0:T(8,128)}, f32[16,160]{1,0:T(8,128)S(1)}, u32[]{:S(2)}) copy-start(f32[16,160]{1,0:T(8,128)S(1)} %select_reduce_fusion.3) | copy-start | bytes 30724
  265.4 330.5 %copy-start.34 = (s32[16,512]{1,0:T(8,128)}, s32[16,512]{1,0:T(8,128)S(1)}, u32[]{:S(2)}) copy-start(s32[16,512]{1,0:T(8,128)S(1)} %fusion.79) | copy-start | bytes 98308
  268.6 142.2 %copy-start.54 = (f32[16,160]{1,0:T(8,128)}, f32[16,160]{1,0:T(8,128)S(1)}, u32[]{:S(2)}) copy-start(f32[16,160]{1,0:T(8,128)S(1)} %select_reduce_fusion.2) | copy-start | bytes 30724
  449.1 146.8 %copy-start.69 = (f32[512]{0:T(512)}, f32[512]{0:T(512)S(1)}, u32[]{:S(2)}) copy-start(f32[512]{0:T(512)S(1)} %add_rsqrt_fusion.2) | copy-start | bytes 6148
  648.6 20.2 %slice-start.7 = ((s8[10485760]{0:T(1024)(128)(4,1)}), s8[4194304]{0:T(1024)(128)(4,1)S(1)}, s32[]{:S(2)}) async-start(s8[10485760]{0:T(1024)(128)(4,1)} %bitcast.299), calls=%async_computation.9 | async-start | bytes 8388608
  648.6 20.2 %slice-start.8 = ((s8[10485760]{0:T(1024)(128)(4,1)}), s8[4194304]{0:T(1024)(128)(4,1)S(1)}, s32[]{:S(2)}) async-start(s8[10485760]{0:T(1024)(128)(4,1)} %bitcast.299), calls=%async_computation.10 | async-start | bytes 8388608
  679.2 80.2 %copy-start.19 = (bf16[2560,384]{0,1:T(8,128)(2,1)}, bf16[2560,384]{0,1:T(8,128)(2,1)S(1)}, u32[]{:S(2)}) copy-start(bf16[2560,384]{0,1:T(8,128)(2,1)S(1)} %get-tuple-element.58) | copy-start | bytes 5898244
  680.5 21.9 %slice-start.4 = ((s8[10485760]{0:T(1024)(128)(4,1)}), s8[4194304]{0:T(1024)(128)(4,1)S(1)}, s32[]{:S(2)}) async-start(s8[10485760]{0:T(1024)(128)(4,1)} %bitcast.295), calls=%async_computation.6 | async-start | bytes 8388608
  680.5 21.9 %slice-start.5 = ((s8[10485760]{0:T(1024)(128)(4,1)}), s8[4194304]{0:T(1024)(128)(4,1)S(1)}, s32[]{:S(2)}) async-start(s8[10485760]{0:T(1024)(128)(4,1)} %bitcast.295), calls=%async_computation.7 | async-start | bytes 8388608
  742.6 16.8 %slice-start.10 = ((s8[10485760]{0:T(1024)(128)(4,1)}), s8[4194304]{0:T(1024)(128)(4,1)S(1)}, s32[]{:S(2)}) async-start(s8[10485760]{0:T(1024)(128)(4,1)} %bitcast.306), calls=%async_computation.12 | async-start | bytes 8388608
  742.7 16.8 %slice-start.11 = ((s8[10485760]{0:T(1024)(128)(4,1)}), s8[4194304]{0:T(1024)(128)(4,1)S(1)}, s32[]{:S(2)}) async-start(s8[10485760]{0:T(1024)(128)(4,1)} %bitcast.306), calls=%async_computation.13 | async-start | bytes 8388608
  975.9 13.7 copy-start.21
  975.9 13.7 copy-start.28
  989.6 12.4 copy-start.44
  989.6 12.4 copy-start.46
  (82 other events, 545.2 us)
Sparse Core Ops, SparseCore 0:
  246.6 28.3 all-reduce.6
  1349.0 25.6 all-reduce.8
